TPU v7x, 128 devices: a whole 4x4x4 slice. The times are simulated.
128 devices in a mesh: rep: 1, r: 16 (over y, z), s: 8 (over x, core).
Axes of the slice: x: 4, y: 4, z: 4, core: 2. Of those that a mesh axis runs over, the one named last changes fastest.
Arguments:
- x: bfloat16 [128, 2048, 1280], P(('rep', 'r', 's'))
- dy: bfloat16 [128, 2048, 1280], P(('rep', 'r', 's'))
- w_gate: bfloat16 [2, 1280, 3584], P(None, 's')
- w_up: bfloat16 [2, 1280, 3584], P(None, 's')
- w_down: bfloat16 [2, 3584, 1280], P(None, 's')
- m_w_gate: float32 [2, 1280, 3584], P(None, 's')
- m_w_up: float32 [2, 1280, 3584], P(None, 's')
- m_w_down: float32 [2, 3584, 1280], P(None, 's')
- v_w_gate: float32 [2, 1280, 3584], P(None, 's')
- v_w_up: float32 [2, 1280, 3584], P(None, 's')
- v_w_down: float32 [2, 3584, 1280], P(None, 's')
Outputs:
- output 1: bfloat16 [2, 1280, 3584], P('rep', 's')
- output 2: bfloat16 [2, 1280, 3584], P('rep', 's')
- output 3: bfloat16 [2, 3584, 1280], P('rep', 's')
- output 4: float32 [2, 1280, 3584], P('rep', 's')
- output 5: float32 [2, 1280, 3584], P('rep', 's')
- output 6: float32 [2, 3584, 1280], P('rep', 's')
- output 7: float32 [2, 1280, 3584], P('rep', 's')
- output 8: float32 [2, 1280, 3584], P('rep', 's')
- output 9: float32 [2, 3584, 1280], P('rep', 's')
All inputs are finite; a program needn't handle non-finite values.
Results may differ from a plain program's by a relative error of at most 0.022.
Values are sent between devices in bfloat16 or wider.
A program may use at most 1.5 GiB of HBM per device.

v0:
```python
import jax
import jax.numpy as jnp
from jax import lax
from jax.sharding import PartitionSpec as P

NAMES = ("w_gate", "w_up", "w_down")


def matmul(a, w):
    return jnp.dot(a, w, preferred_element_type=jnp.float32).astype(jnp.bfloat16)


def normed(h):
    wide = h.astype(jnp.float32)
    scale = lax.rsqrt(jnp.mean(wide**2, -1, keepdims=True) + 1e-6)
    return (wide * scale).astype(jnp.bfloat16)


def layer(h, w):
    a = normed(h)
    gate = jnp.dot(a, w["w_gate"], preferred_element_type=jnp.float32)
    up = jnp.dot(a, w["w_up"], preferred_element_type=jnp.float32)
    return h + matmul((jax.nn.silu(gate) * up).astype(jnp.bfloat16), w["w_down"])


def adamw(w, m, v, g):
    m = 0.9 * m + 0.1 * g
    v = 0.95 * v + 0.05 * g * g
    step = m * lax.rsqrt(v + 1e-8) + 0.1 * w
    return (w - 0.02 * step).astype(jnp.bfloat16), m, v


def clipped(gradients, sum_of_squares, count):
    factor = jnp.minimum(1.0, 0.5 * lax.rsqrt(sum_of_squares / count + 1e-30))
    return [g * factor for g in gradients]


def solution(mesh):
    def fetched(weights, number):
        return {name: lax.all_gather(w[number], "s", axis=0, tiled=True) for name, w in zip(NAMES, weights, strict=True)}

    def summed(term):
        return lax.psum(lax.psum_scatter(term, "s", scatter_dimension=0, tiled=True), "r")

    def step(x, dy, *arrays):
        weights, m, v = (arrays[i : i + 3] for i in (0, 3, 6))
        layers = weights[0].shape[0]
        h, kept = x[0], []
        for number in range(layers):
            kept.append(h)
            h = layer(h, fetched(weights, number))
        by_h, mine = dy[0], [None] * layers
        for number in reversed(range(layers)):
            _, back = jax.vjp(lambda w, h: layer(h, w), fetched(weights, number), kept[number])
            by_w, by_h = back(by_h)
            mine[number] = [summed(by_w[name]) for name in NAMES]
        gradients = [jnp.stack([mine[number][i] for number in range(layers)]).astype(jnp.float32) for i in range(3)]
        squares = lax.psum(sum(jnp.sum(g * g) for g in gradients), "s")
        gradients = clipped(gradients, squares, lax.psum(1, "s") * sum(g.size for g in gradients))
        new = [adamw(w.astype(jnp.float32), m, v, g) for w, m, v, g in zip(weights, m, v, gradients, strict=True)]
        return tuple(one[which] for which in range(3) for one in new)

    states, cut = P(("rep", "r", "s"), None, None), P(None, "s", None)
    return jax.shard_map(
        step,
        mesh=mesh,
        in_specs=(states, states) + (cut,) * 9,
        out_specs=(P("rep", "s", None),) * 9,
        check_vma=False,
    )
```

profile of v0, /device:TPU:1, one launch (start us, length us, event | category | flops | bytes accessed | tf_op | source)
XLA Modules:
  0.0 1017.3 jit_solution(10160086180785589697)
XLA Ops:
  36.6 30.5 %all-gather.13.cloned.1.call-done = bf16[1,1280,3584]{2,1,0:T(8,128)(2,1)} async-done(((bf16[1,160,3584]{2,1,0:T(8,128)(2,1)}), bf16[1,1280,3584]{2,1,0:T(8,128)(2,1)}) %all-gather.13.cloned.1.call-update) | async-done | bytes 9175056 | tf_op jit(solution)/shard_map/all_gather | solution.py:40
  67.1 27.0 %fusion.39 = f32[2048,3584]{1,0:T(8,128)} fusion(bf16[1,1280,3584]{2,1,0:T(8,128)(2,1)} %all-gather.13.cloned.1.call-done, bf16[1,2048,1280]{1,2,0:T(8,128)(2,1)} %copy.20, f32[2048]{0:T(1024)S(1)} %add_rsqrt_fusion), kind=kOutput, calls=%fused_computation.58 | convolution fusion | flops 18798346240 | bytes 43786240 | tf_op jit(solution)/shard_map/dot_general | solution.py:21
  94.1 28.4 %all-gather.15.cloned.1.call-done = bf16[1,1280,3584]{2,1,0:T(8,128)(2,1)} async-done(((bf16[1,160,3584]{2,1,0:T(8,128)(2,1)}), bf16[1,1280,3584]{2,1,0:T(8,128)(2,1)}) %all-gather.15.cloned.1.call-update) | async-done | bytes 9175056 | tf_op jit(solution)/shard_map/all_gather | solution.py:40
  122.5 36.4 %multiply_convert_fusion.1 = (bf16[2048,3584]{1,0:T(8,128)(2,1)}, f32[2048,3584]{1,0:T(8,128)}) fusion(f32[2048,3584]{1,0:T(8,128)} %fusion.39, bf16[1,1280,3584]{2,1,0:T(8,128)(2,1)} %all-gather.15.cloned.1.call-done, bf16[1,2048,1280]{1,2,0:T(8,128)(2,1)} %copy.20, f32[2048]{0:T(1024)S(1)} %add_rsqrt_fusion), kind=kOutput, calls=%fused_computation.17 | convolution fusion | flops 18842386432 | bytes 87826432 | tf_op jit(solution)/shard_map/dot_general | solution.py:22
  177.9 27.0 %fusion.23 = (f32[2048]{0:T(1024)S(1)}, bf16[2048,1280]{0,1:T(8,128)(2,1)}) fusion(bf16[2048,3584]{1,0:T(8,128)(2,1)} %get-tuple-element.30, bf16[1,3584,1280]{2,1,0:T(8,128)(2,1)} %all-gather.17.cloned.1.call-done, bf16[1,2048,1280]{1,2,0:T(8,128)(2,1)} %copy.20), kind=kOutput, calls=%fused_computation.42 | convolution fusion | flops 18803587072 | bytes 34349056 | tf_op jit(solution)/shard_map/dot_general | solution.py:10
  205.5 27.6 %all-gather.21.cloned.1.call-done = bf16[1,3584,1280]{2,1,0:T(8,128)(2,1)} async-done(((bf16[1,448,1280]{2,1,0:T(8,128)(2,1)}), bf16[1,3584,1280]{2,1,0:T(8,128)(2,1)}) %all-gather.21.cloned.1.call-update) | async-done | bytes 9175056 | tf_op jit(solution)/shard_map/all_gather | solution.py:40
  233.1 26.0 %convolution_convert_fusion.4 = bf16[2048,3584]{1,0:T(8,128)(2,1)} fusion(bf16[1,3584,1280]{2,1,0:T(8,128)(2,1)} %all-gather.21.cloned.1.call-done, bf16[1,2048,1280]{2,1,0:T(8,128)(2,1)} %param.12), kind=kOutput, calls=%fused_computation.33 | convolution fusion | flops 18797821952 | bytes 29097984 | tf_op jit(solution)/shard_map/transpose(jvp())/dot_general | solution.py:10
  259.2 29.2 %all-gather.23.cloned.1.call-done = bf16[1,1280,3584]{2,1,0:T(8,128)(2,1)} async-done(((bf16[1,160,3584]{2,1,0:T(8,128)(2,1)}), bf16[1,1280,3584]{2,1,0:T(8,128)(2,1)}) %all-gather.23.cloned.1.call-update) | async-done | bytes 9175056 | tf_op jit(solution)/shard_map/all_gather | solution.py:40
  288.4 27.3 %fusion.26 = f32[2048,3584]{1,0:T(8,128)} fusion(bf16[1,1280,3584]{2,1,0:T(8,128)(2,1)} %all-gather.23.cloned.1.call-done, bf16[2048,1280]{0,1:T(8,128)(2,1)} %get-tuple-element.33, f32[2048]{0:T(1024)S(1)} %fusion.89), kind=kOutput, calls=%fused_computation.45 | convolution fusion | flops 18798346240 | bytes 43786240 | tf_op jit(solution)/shard_map/jvp()/dot_general | solution.py:22
  315.7 27.9 %all-gather.19.cloned.1.call-done = bf16[1,1280,3584]{2,1,0:T(8,128)(2,1)} async-done(((bf16[1,160,3584]{2,1,0:T(8,128)(2,1)}), bf16[1,1280,3584]{2,1,0:T(8,128)(2,1)}) %all-gather.19.cloned.1.call-update) | async-done | bytes 9175056 | tf_op jit(solution)/shard_map/all_gather | solution.py:40
  343.6 44.1 %fusion.2 = (bf16[2048,3584]{1,0:T(8,128)(2,1)}, f32[2048,3584]{1,0:T(8,128)}) fusion(f32[2048,3584]{1,0:T(8,128)} %fusion.26, bf16[2048,3584]{1,0:T(8,128)(2,1)} %convolution_convert_fusion.4, bf16[1,1280,3584]{2,1,0:T(8,128)(2,1)} %all-gather.19.cloned.1.call-done, bf16[2048,1280]{0,1:T(8,128)(2,1)} %get-tuple-element.33, f32[2048]{0:T(1024)S(1)} %fusion.89), kind=kOutput, calls=%fused_computation.8 | convolution fusion | flops 18886426624 | bytes 102506496 | tf_op jit(solution)/shard_map/jvp()/dot_general | solution.py:21
  387.7 26.0 %fusion.44 = bf16[2048,1280]{0,1:T(8,128)(2,1)} fusion(bf16[2048,3584]{1,0:T(8,128)(2,1)} %get-tuple-element.34, bf16[1,1280,3584]{2,1,0:T(8,128)(2,1)} %all-gather.19.cloned.1.call-done), kind=kOutput, calls=%fused_computation.61 | convolution fusion | flops 18790481920 | bytes 29097984 | tf_op jit(solution)/shard_map/transpose(jvp())/dot_general | solution.py:21
  413.7 31.8 %fusion.25 = (f32[2048]{0:T(1024)S(1)}, bf16[2048,1280]{0,1:T(8,128)(2,1)}) fusion(bf16[2048,1280]{0,1:T(8,128)(2,1)S(1)} %copy-done.3, bf16[2048,1280]{0,1:T(8,128)(2,1)} %fusion.44, bf16[1,1280,3584]{2,1,0:T(8,128)(2,1)} %all-gather.23.cloned.1.call-done, bf16[2048,3584]{1,0:T(8,128)(2,1)} %convolution_convert_fusion.4, f32[2048,3584]{1,0:T(8,128)} %get-tuple-element.35), kind=kOutput, calls=%fused_computation.44 | convolution fusion | flops 18850248704 | bytes 68952064 | tf_op jit(solution)/shard_map/transpose(jvp())/dot_general | solution.py:22
  457.8 24.8 %convolution_convert_fusion.2 = bf16[3584,1280]{1,0:T(8,128)(2,1)} fusion(bf16[2048,3584]{1,0:T(8,128)(2,1)} %get-tuple-element.30, bf16[2048,1280]{0,1:T(8,128)(2,1)} %fusion.59), kind=kOutput, calls=%fused_computation.31 | convolution fusion | flops 18795069440 | bytes 29097984 | tf_op jit(solution)/shard_map/transpose(jvp())/dot_general | solution.py:10
  482.7 31.1 %convolution_convert_fusion.1 = bf16[3584,1280]{1,0:T(8,128)(2,1)} fusion(f32[2048,3584]{1,0:T(8,128)} %fusion.26, bf16[1,2048,1280]{2,1,0:T(8,128)(2,1)} %param.12, f32[2048,3584]{1,0:T(8,128)} %get-tuple-element.35), kind=kOutput, calls=%fused_computation.30 | convolution fusion | flops 18839109632 | bytes 73138176 | tf_op jit(solution)/shard_map/transpose(jvp())/dot_general | solution.py:10
  514.0 26.3 %convolution_convert_fusion.3 = bf16[2048,3584]{1,0:T(8,128)(2,1)} fusion(bf16[2048,1280]{0,1:T(8,128)(2,1)} %fusion.59, bf16[1,3584,1280]{2,1,0:T(8,128)(2,1)} %all-gather.17.cloned.1.call-done), kind=kOutput, calls=%fused_computation.32 | convolution fusion | flops 18797821952 | bytes 29097984 | tf_op jit(solution)/shard_map/transpose(jvp())/dot_general | solution.py:10
  540.2 30.4 %fusion.17 = bf16[1280,3584]{1,0:T(8,128)(2,1)} fusion(bf16[2048,3584]{1,0:T(8,128)(2,1)} %convolution_convert_fusion.3, f32[2048,3584]{1,0:T(8,128)} %fusion.39, bf16[1,2048,1280]{1,2,0:T(8,128)(2,1)} %copy.20, f32[2048]{0:T(1024)S(1)} %copy-done.11), kind=kOutput, calls=%fused_computation.29 | convolution fusion | flops 18846973952 | bytes 58466304 | tf_op jit(solution)/shard_map/transpose(jvp())/dot_general | solution.py:22
  571.3 30.3 %fusion.16 = bf16[1280,3584]{1,0:T(8,128)(2,1)} fusion(bf16[2048,3584]{1,0:T(8,128)(2,1)} %convolution_convert_fusion.4, bf16[2048,1280]{0,1:T(8,128)(2,1)} %get-tuple-element.33, f32[2048]{0:T(1024)S(1)} %copy-done.7, f32[2048,3584]{1,0:T(8,128)} %get-tuple-element.35), kind=kOutput, calls=%fused_computation.28 | convolution fusion | flops 18846973952 | bytes 58466304 | tf_op jit(solution)/shard_map/transpose(jvp())/dot_general | solution.py:22
  601.6 37.0 %fusion.13 = bf16[1280,3584]{1,0:T(8,128)(2,1)} fusion(f32[2048,3584]{1,0:T(8,128)} %fusion.39, f32[2048,3584]{1,0:T(8,128)} %get-tuple-element.31, bf16[2048,3584]{1,0:T(8,128)(2,1)} %convolution_convert_fusion.3, bf16[1,2048,1280]{1,2,0:T(8,128)(2,1)} %copy.20, f32[2048]{0:T(1024)S(1)} %copy-done.11), kind=kOutput, calls=%fused_computation.26 | convolution fusion | flops 18883674112 | bytes 87826432 | tf_op jit(solution)/shard_map/transpose(jvp())/dot_general | solution.py:21
  638.7 26.4 %convolution_convert_fusion = bf16[1280,3584]{1,0:T(8,128)(2,1)} fusion(bf16[2048,3584]{1,0:T(8,128)(2,1)} %get-tuple-element.34, bf16[2048,1280]{0,1:T(8,128)(2,1)} %get-tuple-element.33, f32[2048]{0:T(1024)S(1)} %copy-done.7), kind=kOutput, calls=%fused_computation.27 | convolution fusion | flops 18798346240 | bytes 29106176 | tf_op jit(solution)/shard_map/transpose(jvp())/dot_general | solution.py:21
  665.2 48.2 %reduce-scatter.13.cloned.1.call-done = bf16[160,3584]{1,0:T(8,128)(2,1)} async-done(((bf16[1280,3584]{1,0:T(8,128)(2,1)}), bf16[160,3584]{1,0:T(8,128)(2,1)}) %reduce-scatter.13.cloned.1.call-update) | async-done | bytes 1146896 | tf_op jit(solution)/shard_map/reduce_scatter | solution.py:43
  713.5 58.4 %reduce-scatter.7.cloned.1.call-done = bf16[160,3584]{1,0:T(8,128)(2,1)} async-done(((bf16[1280,3584]{1,0:T(8,128)(2,1)}), bf16[160,3584]{1,0:T(8,128)(2,1)}) %reduce-scatter.7.cloned.1.call-update) | async-done | bytes 1146896 | tf_op jit(solution)/shard_map/reduce_scatter | solution.py:43
  771.9 58.2 %reduce-scatter.9.cloned.1.call-done = bf16[160,3584]{1,0:T(8,128)(2,1)} async-done(((bf16[1280,3584]{1,0:T(8,128)(2,1)}), bf16[160,3584]{1,0:T(8,128)(2,1)}) %reduce-scatter.9.cloned.1.call-update) | async-done | bytes 1146896 | tf_op jit(solution)/shard_map/reduce_scatter | solution.py:43
  830.1 131.7 %all-reduce.3.cloned.1.call-done = (bf16[1,160,3584]{2,1,0:T(8,128)(2,1)}, bf16[1,160,3584]{2,1,0:T(8,128)(2,1)}, bf16[1,160,3584]{2,1,0:T(8,128)(2,1)}, bf16[1,...) async-done(((bf16[1,160,3584]{2,1,0:T(8,128)(2,1)}, bf16[1,160,3584]{2,1,0:T(8,128)(2,1)}, bf16[1,160,3584]{2,1,0:T(8,128)(2,1)}, ...) | async-done | bytes 6881296 | tf_op jit(solution)/shard_map/psum | solution.py:43
  (70 shorter events, 108.1 us)
Async XLA Ops:
  7.2 3.4 copy-start.1
  7.2 59.9 %all-gather.13.cloned.1.call-start = ((), (), s32[]{:S(2)}) async-start(), calls=%async_computation.12 | async-start | bytes 10321920 | tf_op jit(solution)/shard_map/all_gather | solution.py:40
  10.5 112.0 %all-gather.15.cloned.1.call-start = ((), (), s32[]{:S(2)}) async-start(), calls=%async_computation.13 | async-start | bytes 10321920 | tf_op jit(solution)/shard_map/all_gather | solution.py:40
  12.2 165.7 %all-gather.17.cloned.1.call-start = ((), (), s32[]{:S(2)}) async-start(), calls=%async_computation.14 | async-start | bytes 10321920 | tf_op jit(solution)/shard_map/all_gather | solution.py:40
  15.4 217.8 %all-gather.21.cloned.1.call-start = ((), (), s32[]{:S(2)}) async-start(), calls=%async_computation.16 | async-start | bytes 10321920 | tf_op jit(solution)/shard_map/all_gather | solution.py:40
  15.9 272.4 %all-gather.23.cloned.1.call-start = ((), (), s32[]{:S(2)}) async-start(), calls=%async_computation.17 | async-start | bytes 10321920 | tf_op jit(solution)/shard_map/all_gather | solution.py:40
  16.5 327.1 %all-gather.19.cloned.1.call-start = ((), (), s32[]{:S(2)}) async-start(), calls=%async_computation.15 | async-start | bytes 10321920 | tf_op jit(solution)/shard_map/all_gather | solution.py:40
  17.1 648.1 %reduce-scatter.15.cloned.1.call-start = ((), (), s32[]{:S(2)}) async-start(), calls=%async_computation.10 | async-start | bytes 10321920 | tf_op jit(solution)/shard_map/reduce_scatter | solution.py:43
  28.7 93.8 %copy-start.10 = (f32[2048]{0:T(1024)}, f32[2048]{0:T(1024)S(1)}, u32[]{:S(2)}) copy-start(f32[2048]{0:T(1024)S(1)} %add_rsqrt_fusion) | copy-start | bytes 24580
  205.5 240.0 %copy-start.6 = (f32[2048]{0:T(1024)}, f32[2048]{0:T(1024)S(1)}, u32[]{:S(2)}) copy-start(f32[2048]{0:T(1024)S(1)} %fusion.89) | copy-start | bytes 24580
  387.7 26.0 %copy-start.3 = (bf16[2048,1280]{0,1:T(8,128)(2,1)S(1)}, bf16[2048,1280]{0,1:T(8,128)(2,1)}, u32[]{:S(2)}) copy-start(bf16[2048,1280]{0,1:T(8,128)(2,1)} %get-tuple-element.33) | copy-start | bytes 15728644
  413.7 31.8 %copy-start.9 = (f32[2048]{0:T(1024)S(1)}, f32[2048]{0:T(1024)}, u32[]{:S(2)}) copy-start(f32[2048]{0:T(1024)} %copy-done.8) | copy-start | bytes 24580
  482.7 182.5 %reduce-scatter.17.cloned.1.call-start = ((), (), s32[]{:S(2)}) async-start(), calls=%async_computation.11 | async-start | bytes 10321920 | tf_op jit(solution)/shard_map/reduce_scatter | solution.py:43
  513.9 26.3 %copy-start.11 = (f32[2048]{0:T(1024)S(1)}, f32[2048]{0:T(1024)}, u32[]{:S(2)}) copy-start(f32[2048]{0:T(1024)} %copy-done.10) | copy-start | bytes 24580
  513.9 151.3 %reduce-scatter.11.cloned.1.call-start = ((), (), s32[]{:S(2)}) async-start(), calls=%async_computation.8 | async-start | bytes 10321920 | tf_op jit(solution)/shard_map/reduce_scatter | solution.py:43
  570.6 0.7 copy-start.7
  570.6 142.9 %reduce-scatter.13.cloned.1.call-start = ((), (), s32[]{:S(2)}) async-start(), calls=%async_computation.9 | async-start | bytes 10321920 | tf_op jit(solution)/shard_map/reduce_scatter | solution.py:43
  601.6 170.3 %reduce-scatter.7.cloned.1.call-start = ((), (), s32[]{:S(2)}) async-start(), calls=%async_computation.6 | async-start | bytes 10321920 | tf_op jit(solution)/shard_map/reduce_scatter | solution.py:43
  638.7 191.4 %reduce-scatter.9.cloned.1.call-start = ((), (), s32[]{:S(2)}) async-start(), calls=%async_computation.7 | async-start | bytes 10321920 | tf_op jit(solution)/shard_map/reduce_scatter | solution.py:43
  665.1 296.7 %all-reduce.3.cloned.1.call-start = ((), (), s32[]{:S(2)}) async-start(), calls=%async_computation.18 | async-start | bytes 13762560 | tf_op jit(solution)/shard_map/psum | solution.py:43
  961.8 6.9 copy-start.4
  961.8 6.9 copy-start.5
  986.6 9.1 copy-start
  986.6 9.1 copy-start.2
  (1 other events, 0.6 us)
Sparse Core Ops, SparseCore 0:
  10.7 56.3 all-gather.12
  69.4 53.0 all-gather.14
  124.8 53.0 all-gather.16
  180.0 53.0 all-gather.20
  235.3 53.0 all-gather.22
  290.5 53.0 all-gather.18
  482.8 55.6 reduce-scatter.14
  540.9 55.9 reduce-scatter.16
  599.3 55.9 reduce-scatter.10
  657.5 55.9 reduce-scatter.12
  715.9 55.9 reduce-scatter.6
  774.2 55.9 reduce-scatter.8
  834.4 127.3 all-reduce.2
where the time goes:
time: 1030 us; the launch traced here: 1020 us
  waiting for transfers between devices  461 us (45%)
  matrix products  452 us (44%)
  other arithmetic  48.3 us (5%)
  local copies, waits for them, and re-layouts  25.1 us (2%)
  between operations  17.1 us (2%)
  blocking collectives  13.4 us (1%)
    reduce_scatter x6, waiting for transfers between devices, summed(): lax.psum_scatter(term, 's', scatter_dimension=0, tiled=True)  165 us
    all_gather x6, waiting for transfers between devices, fetched(): lax.all_gather(w[number], 's', axis=0, tiled=True)  163 us
    dot_general x5, matrix products, layer(): gate = jnp.dot(a, w['w_gate'], preferred_element_type=jnp.float32)  160 us
    dot_general x5, matrix products, layer(): up = jnp.dot(a, w['w_up'], preferred_element_type=jnp.float32)  156 us
    dot_general x5, matrix products, matmul(): jnp.dot(a, w, preferred_element_type=jnp.float32).astype(jnp.bfloat16)  135 us
    psum x1, waiting for transfers between devices, summed(): lax.psum(lax.psum_scatter(term, 's', scatter_dimension=0, tiled=True), 'r')  132 us
    convert_element_type x2, other arithmetic, adamw(): return ((w - 0.02 * step).astype(jnp.bfloat16), m, v)  23.7 us
  transfers between devices with their start and end apart: 13, of which 10 were waited for; matrix products, arithmetic and copies ran while one was open for 34% of the time, Pallas kernels for 0%

commit v1 on v0

v1 whole, which is shorter than its diff:
```python
import functools

import jax
import jax.numpy as jnp
from jax import lax
from jax.experimental import pallas as pl
from jax.experimental.pallas import tpu as pltpu
from jax.sharding import PartitionSpec as P

bf16, f32 = jnp.bfloat16, jnp.float32
MESH = pl.DeviceIdType.MESH
VMEM_ALL = 67043328
ORDERS = ((0, 1, 2), (1, 2, 0), (2, 0, 1))


class Place:
    def __init__(self):
        rep, r, s = lax.axis_index("rep"), lax.axis_index("r"), lax.axis_index("s")
        self.rep = rep
        self.c = lax.rem(s, 2)
        self.at = (s // 2, r // 4, lax.rem(r, 4))

    def id(self, x, y, z, c):
        return (self.rep, y * 4 + z, x * 2 + c)

    def along(self, axis, k):
        at = list(self.at)
        at[axis] = lax.rem(at[axis] + k, 4)
        return at[axis], self.id(*at, self.c)

    def partner(self):
        return self.id(*self.at, 1 - self.c)

    def meet(self, more=()):
        barrier = pltpu.get_barrier_semaphore()
        ids = [self.partner()] + [self.along(a, k)[1] for a in range(3) for k in (1, 2, 3)] + list(more)
        for i in ids:
            pl.semaphore_signal(barrier, inc=1, device_id=i, device_id_type=MESH)
        pl.semaphore_wait(barrier, len(ids))


def arrive(ref, sem):
    pltpu.make_async_copy(ref, ref, sem).wait()


def send(src, dst, send_sem, recv_sem, to):
    pltpu.make_async_remote_copy(src_ref=src, dst_ref=dst, send_sem=send_sem, recv_sem=recv_sem, device_id=to, device_id_type=MESH).start()


class Sum:
    def __init__(self, units, rows, cols, parts, ring=None):
        self.units, self.rows, self.cols, self.parts = units, rows, cols, parts
        self.sizes = [(p[0][1], p[1][1]) for p in parts]

    def scratch(self):
        u = self.units
        shapes = dict(s=pltpu.VMEM((u, 4, 4, 4, self.rows, self.cols), bf16), ga=pltpu.VMEM((u, 4, 4, self.rows, self.cols), bf16))
        for k, (r, c) in enumerate(self.sizes):
            shapes[f"p1{k}"] = pltpu.VMEM((u, 3, 4, 4, r, c), bf16)
            shapes[f"o1{k}"] = pltpu.VMEM((u, 4, 4, r, c), f32)
            shapes[f"p2{k}"] = pltpu.VMEM((u, 3, 4, r, c), bf16)
            shapes[f"o2{k}"] = pltpu.VMEM((u, 4, r, c), f32)
            shapes[f"p3{k}"] = pltpu.VMEM((u, 3, r, c), bf16)
        shapes["snd"] = pltpu.SemaphoreType.DMA((5, u, 3))
        shapes["rcv"] = pltpu.SemaphoreType.DMA((5, u, 3))
        return shapes

    def bind(self, place, refs):
        self.place, self.ref = place, refs
        return self

    def cut(self, k):
        (r0, r), (c0, c) = self.parts[k]
        return pl.ds(r0, r), pl.ds(c0, c)

    def own(self, k):
        return self.place.at[ORDERS[k][0]]

    def piece(self, k, q):
        axis = ORDERS[k][0]
        return tuple(q if a == axis else slice(None) for a in range(3))

    def start1(self, u):
        R = self.ref
        for k in range(3):
            for j in (1, 2, 3):
                q, to = self.place.along(ORDERS[k][0], j)
                send(R["s"].at[(u,) + self.piece(k, q) + self.cut(k)], R[f"p1{k}"].at[u, j - 1], R["snd"].at[0, u, k], R["rcv"].at[0, u, k], to)

    def add1(self, u):
        R = self.ref
        for k in range(3):
            p, o = R[f"p1{k}"], R[f"o1{k}"]
            arrive(p.at[u], R["rcv"].at[0, u, k])

            def some(i, _, p=p, o=o):
                t = o[u, i] + p[u, 0, i].astype(f32) + p[u, 1, i].astype(f32) + p[u, 2, i].astype(f32)
                o[u, i] = t
                p[u, 0, i] = t.astype(bf16)
                return 0

            lax.fori_loop(0, 4, some, 0)
            axis = ORDERS[k][1]
            for j in (1, 2, 3):
                q, to = self.place.along(axis, j)
                at = (u, 0, q) if self.second_is_first(k) else (u, 0, slice(None), q)
                send(p.at[at], R[f"p2{k}"].at[u, j - 1], R["snd"].at[1, u, k], R["rcv"].at[1, u, k], to)

    def second_is_first(self, k):
        left = [a for a in range(3) if a != ORDERS[k][0]]
        return left[0] == ORDERS[k][1]

    def add2(self, u):
        R = self.ref
        for k in range(3):
            p, o1, o = R[f"p2{k}"], R[f"o1{k}"], R[f"o2{k}"]
            arrive(p.at[u], R["rcv"].at[1, u, k])
            me = self.place.at[ORDERS[k][1]]
            for i in range(4):
                mine = o1[u, me, i] if self.second_is_first(k) else o1[u, i, me]
                t = mine + p[u, 0, i].astype(f32) + p[u, 1, i].astype(f32) + p[u, 2, i].astype(f32)
                o[u, i] = t
                p[u, 0, i] = t.astype(bf16)
            for j in (1, 2, 3):
                q, to = self.place.along(ORDERS[k][2], j)
                send(p.at[u, 0, q], R[f"p3{k}"].at[u, j - 1], R["snd"].at[2, u, k], R["rcv"].at[2, u, k], to)

    def first(self, k):
        return 1 if k != 1 else 2

    def add3(self, u):
        R = self.ref
        _, y, z = self.place.at
        for k in range(3):
            p, o = R[f"p3{k}"], R[f"o2{k}"]
            arrive(p.at[u], R["rcv"].at[2, u, k])
            t = o[u, self.place.at[ORDERS[k][2]]] + p[u, 0].astype(f32) + p[u, 1].astype(f32) + p[u, 2].astype(f32)
            (r0, r), (c0, c) = self.parts[k]
            R["ga"][u, y, z, r0 : r0 + r, c0 : c0 + c] = t.astype(bf16)
            mine = R["ga"].at[(u, y, z) + self.cut(k)]
            for j in (1, 2, 3):
                _, to = self.place.along(self.first(k), j)
                send(mine, mine, R["snd"].at[3, u, k], R["rcv"].at[3, u, k], to)

    def gather(self, u):
        R = self.ref
        _, y, z = self.place.at
        for k in range(3):
            arrive(R["ga"].at[(u, pl.ds(0, 3), 0) + self.cut(k)], R["rcv"].at[3, u, k])
            at = (u, slice(None), z) if self.first(k) == 1 else (u, y, slice(None))
            line = R["ga"].at[at + self.cut(k)]
            for j in (1, 2, 3):
                _, to = self.place.along(3 - self.first(k), j)
                send(line, line, R["snd"].at[4, u, k], R["rcv"].at[4, u, k], to)

    def gathered(self, u):
        R = self.ref
        for k in range(3):
            arrive(R["ga"].at[(u, pl.ds(0, 3), slice(None)) + self.cut(k)], R["rcv"].at[4, u, k])

    def finish(self):
        R = self.ref

        def one(u, _):
            for k in range(3):
                arrive(R[f"p1{k}"].at[u], R["snd"].at[0, u, k])
                arrive(R[f"p2{k}"].at[u], R["snd"].at[1, u, k])
                arrive(R[f"p3{k}"].at[u], R["snd"].at[2, u, k])
                arrive(R["ga"].at[(u, pl.ds(0, 3), 0) + self.cut(k)], R["snd"].at[3, u, k])
                arrive(R["ga"].at[(u, pl.ds(0, 3), slice(None)) + self.cut(k)], R["snd"].at[4, u, k])
            return 0

        lax.fori_loop(0, self.units, one, 0)

    def stages(self, t):
        for lag, stage in ((2, self.add1), (3, self.add2), (4, self.add3), (5, self.gather), (6, self.gathered)):
            u = t - lag

            @pl.when((u >= 0) & (u < self.units))
            def _(stage=stage, u=u):
                stage(u)


GU = Sum(7, 80, 128, (((0, 32), (0, 128)), ((32, 32), (0, 128)), ((64, 16), (0, 128))))
DOWN = Sum(1, 56, 640, (((0, 56), (0, 256)), ((0, 56), (256, 256)), ((0, 56), (512, 128))))


def own_parts(rs, u, oh, x=None):
    R = rs.ref
    for k in range(3):
        me = rs.own(k)
        (r0, r), (c0, c) = rs.parts[k]
        for i in range(4):
            for j in range(4):
                rest = [i, j]
                at = tuple(me if a == ORDERS[k][0] else rest.pop(0) for a in range(3))
                yield k, i, j, at, (slice(r0, r0 + r), slice(c0, c0 + c))


def gu_halves(rs, u, slot, oh, d2d):
    R = rs.ref
    arrive(R["s"].at[u], d2d.at[u])
    for k in range(3):
        me = rs.own(k)
        (r0, r), (c0, c) = rs.parts[k]

        def some(i, _, k=k, me=me, r0=r0, r=r):
            for j in range(4):
                rest = [i, j]
                at = tuple(me if a == ORDERS[k][0] else rest.pop(0) for a in range(3))
                R[f"o1{k}"][u, i, j] = oh[(slot,) + at + (slice(r0, r0 + r),)] + R["s"][(u,) + at + (slice(r0, r0 + r),)].astype(f32)
            return 0

        lax.fori_loop(0, 4, some, 0)

    def all_of(i, _):
        x, y = i // 4, lax.rem(i, 4)
        for z in range(4):
            R["s"][u, x, y, z] = (oh[slot, x, y, z] + R["s"][u, x, y, z].astype(f32)).astype(bf16)
        return 0

    lax.fori_loop(0, 16, all_of, 0)
    rs.start1(u)


def gu_kernel(aT, dg, du, ga_out, *scratch, names):
    refs = dict(zip(names, scratch, strict=True))
    place = Place()
    c = place.c
    rs = GU.bind(place, refs)
    a, r, oh, sb, asem, rsem, d2d_s, d2d_r, osem = (refs[n] for n in ("a", "r", "oh", "sb", "asem", "rsem", "d2d_s", "d2d_r", "osem"))

    def chunk(m, j, slot):
        src = (dg, du)[m]
        return pltpu.make_async_copy(src.at[:, pl.ds(pl.multiple_of(j * 512, 512), 512)], r.at[slot, m], rsem.at[slot, m])

    for h in range(2):
        pltpu.make_async_copy(aT.at[:, 1 - c if h == 0 else c], a.at[h], asem.at[h]).start()
    for m in range(2):
        chunk(m, 0, 0).start()
    place.meet()
    for h in range(2):
        arrive(a.at[h], asem.at[h])

    def step(t, _):
        slot = lax.rem(t, 2)

        @pl.when(t < 7)
        def _():
            @pl.when(t + 1 < 7)
            def _():
                for m in range(2):
                    chunk(m, t + 1, 1 - slot).start()

            @pl.when(t >= 2)
            def _():
                arrive(sb.at[slot], d2d_s.at[slot])

            for m in range(2):
                chunk(m, t, slot).wait()
                res = jnp.dot(a[...].reshape(1280, 2048), r[slot, m], preferred_element_type=f32)
                for x in range(4):
                    for h in range(2):
                        for y in range(4):
                            row = x * 160 + h * 80
                            sb[slot, x, y, 2 * m + h] = res[row : row + 80, y * 128 : y * 128 + 128].astype(bf16)
                            oh[slot, x, y, 2 * m + h] = res[640 + row : 640 + row + 80, y * 128 : y * 128 + 128]
            send(sb.at[slot], refs["s"].at[t], d2d_s.at[slot], d2d_r.at[t], place.partner())

        @pl.when((t >= 1) & (t < 8))
        def _():
            gu_halves(rs, t - 1, 1 - slot, oh, d2d_r)

        rs.stages(t)
        return 0

    lax.fori_loop(0, 13, step, 0)
    for slot in range(2):
        arrive(sb.at[slot], d2d_s.at[slot])
    rs.finish()
    out = pltpu.make_async_copy(refs["ga"], ga_out, osem)
    out.start()
    out.wait()


def gu_grads(aT, dg, du, collective_id):
    scratch = GU.scratch()
    scratch.update(
        a=pltpu.VMEM((2, 4, 160, 2048), bf16),
        r=pltpu.VMEM((2, 2, 2048, 512), bf16),
        oh=pltpu.VMEM((2, 4, 4, 4, 80, 128), f32),
        sb=pltpu.VMEM((2, 4, 4, 4, 80, 128), bf16),
        asem=pltpu.SemaphoreType.DMA((2,)),
        rsem=pltpu.SemaphoreType.DMA((2, 2)),
        d2d_s=pltpu.SemaphoreType.DMA((2,)),
        d2d_r=pltpu.SemaphoreType.DMA((7,)),
        osem=pltpu.SemaphoreType.DMA,
    )
    out = pl.pallas_call(
        functools.partial(gu_kernel, names=tuple(scratch)),
        out_shape=jax.ShapeDtypeStruct((7, 4, 4, 80, 128), bf16),
        in_specs=[pl.BlockSpec(memory_space=pl.ANY)] * 3,
        out_specs=pl.BlockSpec(memory_space=pl.ANY),
        scratch_shapes=list(scratch.values()),
        compiler_params=pltpu.CompilerParams(collective_id=collective_id, has_side_effects=True, vmem_limit_bytes=VMEM_ALL),
        name="gu_grads",
    )(aT.reshape(4, 2, 160, 2048), dg, du)
    out = out.reshape(7, 4, 2, 2, 80, 128).transpose(2, 3, 4, 0, 1, 5).reshape(2, 160, 3584)
    return out[0], out[1]


def down_half(rs, x, slot, oh, d2d):
    R = rs.ref
    arrive(R["s"].at[0, x], d2d.at[x])
    xm, ym, zm = rs.place.at
    s, (c0, c1, c2) = R["s"], [slice(p[1][0], p[1][0] + p[1][1]) for p in rs.parts]
    for i in range(4):
        R["o11"][0, x, i] = oh[slot, ym, i, :, c1] + s[0, x, ym, i, :, c1].astype(f32)
        R["o12"][0, x, i] = oh[slot, i, zm, :, c2] + s[0, x, i, zm, :, c2].astype(f32)

    @pl.when(x == xm)
    def _():
        for i in range(4):
            for j in range(4):
                R["o10"][0, i, j] = oh[slot, i, j, :, c0] + s[0, x, i, j, :, c0].astype(f32)

    def all_of(y, _):
        for z in range(4):
            s[0, x, y, z] = (oh[slot, y, z] + s[0, x, y, z].astype(f32)).astype(bf16)
        return 0

    lax.fori_loop(0, 4, all_of, 0)


def down_kernel(hid, dy, ga_out, *scratch, names):
    refs = dict(zip(names, scratch, strict=True))
    place = Place()
    rs = DOWN.bind(place, refs)
    l, d, t_ref, oh, sb, lsem, dsem, d2d_s, d2d_r, osem = (refs[n] for n in ("l", "d", "t", "oh", "sb", "lsem", "dsem", "d2d_s", "d2d_r", "osem"))

    def chunk(x, slot):
        return pltpu.make_async_copy(hid.at[:, pl.ds(pl.multiple_of(x * 896, 128), 896)], l.at[slot], lsem.at[slot])

    whole = pltpu.make_async_copy(dy, d, dsem)
    whole.start()
    chunk(0, 0).start()
    place.meet()
    whole.wait()

    def step(x, _):
        slot = lax.rem(x, 2)

        @pl.when(x < 4)
        def _():
            @pl.when(x + 1 < 4)
            def _():
                chunk(x + 1, 1 - slot).start()

            @pl.when(x >= 2)
            def _():
                arrive(sb.at[slot], d2d_s.at[slot])

            chunk(x, slot).wait()
            t_ref[...] = lax.dot_general(l[slot], d[...], (((0,), (0,)), ((), ())), preferred_element_type=f32).reshape(2, 448, 1280)
            for y in range(4):
                for z in range(4):
                    row, col = y * 112 + (z // 2) * 56, (z % 2) * 640
                    sb[slot, y, z] = t_ref[1 - place.c, row : row + 56, col : col + 640].astype(bf16)
                    oh[slot, y, z] = t_ref[place.c, row : row + 56, col : col + 640]
            send(sb.at[slot], refs["s"].at[0, x], d2d_s.at[slot], d2d_r.at[x], place.partner())

        @pl.when(x >= 1)
        def _():
            down_half(rs, x - 1, 1 - slot, oh, d2d_r)

        return 0

    lax.fori_loop(0, 5, step, 0)
    rs.start1(0)
    rs.add1(0)
    rs.add2(0)
    rs.add3(0)
    rs.gather(0)
    rs.gathered(0)
    for slot in range(2):
        arrive(sb.at[slot], d2d_s.at[slot])
    rs.finish()
    out = pltpu.make_async_copy(refs["ga"], ga_out, osem)
    out.start()
    out.wait()


def down_grads(hid, dy, collective_id):
    scratch = DOWN.scratch()
    scratch.update(
        l=pltpu.VMEM((2, 2048, 896), bf16),
        d=pltpu.VMEM((2048, 1280), bf16),
        t=pltpu.VMEM((2, 448, 1280), f32),
        oh=pltpu.VMEM((2, 4, 4, 56, 640), f32),
        sb=pltpu.VMEM((2, 4, 4, 56, 640), bf16),
        lsem=pltpu.SemaphoreType.DMA((2,)),
        dsem=pltpu.SemaphoreType.DMA,
        d2d_s=pltpu.SemaphoreType.DMA((2,)),
        d2d_r=pltpu.SemaphoreType.DMA((4,)),
        osem=pltpu.SemaphoreType.DMA,
    )
    out = pl.pallas_call(
        functools.partial(down_kernel, names=tuple(scratch)),
        out_shape=jax.ShapeDtypeStruct((1, 4, 4, 56, 640), bf16),
        in_specs=[pl.BlockSpec(memory_space=pl.ANY)] * 2,
        out_specs=pl.BlockSpec(memory_space=pl.ANY),
        scratch_shapes=list(scratch.values()),
        compiler_params=pltpu.CompilerParams(collective_id=collective_id, has_side_effects=True, vmem_limit_bytes=VMEM_ALL),
        name="down_grads",
    )(hid, dy)
    return out.reshape(4, 2, 2, 56, 640).transpose(0, 1, 3, 2, 4).reshape(448, 1280)
NAMES = ("w_gate", "w_up", "w_down")


def matmul(a, w):
    return jnp.dot(a, w, preferred_element_type=f32).astype(bf16)


def scale_of(h):
    wide = h.astype(f32)
    return lax.rsqrt(jnp.mean(wide**2, -1, keepdims=True) + 1e-6)


def normed(h, scale):
    return (h.astype(f32) * scale).astype(bf16)


def adamw(w, m, v, g):
    m = 0.9 * m + 0.1 * g
    v = 0.95 * v + 0.05 * g * g
    step = m * lax.rsqrt(v + 1e-8) + 0.1 * w
    return (w - 0.02 * step).astype(bf16), m, v


def clipped(gradients, sum_of_squares, count):
    factor = jnp.minimum(1.0, 0.5 * lax.rsqrt(sum_of_squares / count + 1e-30))
    return [g * factor for g in gradients]


def back_norm(by_a, h, scale):
    by_a, wide = by_a.astype(f32), h.astype(f32)
    along = jnp.mean(by_a * wide, -1, keepdims=True)
    return (by_a * scale - wide * (scale**3 * along)).astype(bf16)


def solution(mesh):
    def fetched(weights, number):
        return [lax.all_gather(w[number], "s", axis=0, tiled=True) for w in weights]

    def step(x, dy, *arrays):
        weights, m, v = (arrays[i : i + 3] for i in (0, 3, 6))
        h, by_y, kept = x[0], dy[0], []
        for number in range(2):
            w_gate, w_up, w_down = fetched(weights, number)
            scale = scale_of(h)
            a = normed(h, scale)
            gate, up = (jnp.dot(a, w, preferred_element_type=f32) for w in (w_gate, w_up))
            hid = (jax.nn.silu(gate) * up).astype(bf16)
            kept.append((h, scale, a, gate, up, hid, w_gate, w_up, w_down))
            h = h + matmul(hid, w_down)
        mine = [None, None]
        for number in (1, 0):
            h, scale, a, gate, up, hid, w_gate, w_up, w_down = kept[number]
            by_hid = matmul(by_y, w_down.T).astype(f32)
            sig = jax.nn.sigmoid(gate)
            by_up = (by_hid * (gate * sig)).astype(bf16)
            by_gate = (by_hid * up * (sig * (1.0 + gate * (1.0 - sig)))).astype(bf16)
            down = down_grads(hid, by_y, 2 * number)
            g, u = gu_grads(a.T, by_gate, by_up, 2 * number + 1)
            mine[number] = (g, u, down)
            if number:
                by_a = matmul(by_gate, w_gate.T) + matmul(by_up, w_up.T)
                by_y = by_y + back_norm(by_a, h, scale)
        gradients = [jnp.stack([mine[number][i] for number in range(2)]).astype(f32) for i in range(3)]
        squares = lax.psum(sum(jnp.sum(g * g) for g in gradients), "s")
        gradients = clipped(gradients, squares, 8 * sum(g.size for g in gradients))
        new = [adamw(w.astype(f32), m, v, g) for w, m, v, g in zip(weights, m, v, gradients, strict=True)]
        return tuple(one[which] for which in range(3) for one in new)

    states, cut = P(("rep", "r", "s"), None, None), P(None, "s", None)
    return jax.shard_map(
        step,
        mesh=mesh,
        in_specs=(states, states) + (cut,) * 9,
        out_specs=(P("rep", "s", None),) * 9,
        check_vma=False,
    )
```

time: 1030 us -> 920 us (0.89)
  Pallas kernels: 0 us -> 332 us
  waiting for transfers between devices: 461 us -> 168 us
  matrix products: 452 us -> 278 us
  local copies, waits for them, and re-layouts: 25.1 us -> 49.7 us
    pallas_call x0 -> x4, Pallas kernels: none -> 332 us  [the longest x2 178 us: gu_grads(): pl.pallas_call(functools.partial(gu_kernel, names=tuple(scratch)), out_sh...]
    dot_general x15 -> x9, matrix products: 452 us -> 278 us  [the longest x5 147 us: matmul(): return jnp.dot(a, w, preferred_element_type=f32).astype(bf16)]
    reduce_scatter x6 -> x0, waiting for transfers between devices: 165 us -> none  [summed(): lax.psum_scatter(term, 's', scatter_dimension=0, tiled=True)]
    psum x1 -> x0, waiting for transfers between devices: 132 us -> none  [summed(): lax.psum(lax.psum_scatter(term, 's', scatter_dimension=0, tiled=True), 'r')]
    transpose x0 -> x4, local copies, waits for them, and re-layouts: none -> 20.3 us  [the longest x2 16 us: step(): g, u = gu_grads(a.T, by_gate, by_up, 2 * number + 1)]
    slice x3 -> x13, local copies, waits for them, and re-layouts: 7.94 us -> 25.6 us  [the longest x10 17.7 us: gu_grads(): return (out[0], out[1])]
    unnamed x26 -> x38, local copies, waits for them, and re-layouts: 17.1 us -> 0.7 us
    add_any x1 -> x0, other arithmetic: 12.3 us -> none  [normed(): wide = h.astype(jnp.float32)]
  transfers between devices with their start and end apart: 13 -> 6, of which waited for: 10 -> 6; matrix products, arithmetic and copies ran while one was open for 34% -> 18% of each run, Pallas kernels for 0% -> 0%
where the time goes in v1:
time: 920 us; the launch traced here: 916 us
  Pallas kernels  332 us (36%)
  matrix products  278 us (30%)
  waiting for transfers between devices  168 us (18%)
  other arithmetic  52.5 us (6%)
  local copies, waits for them, and re-layouts  49.7 us (5%)
  blocking collectives  18.5 us (2%)
  between operations  17.6 us (2%)
    pallas_call x2, Pallas kernels, gu_grads(): pl.pallas_call(functools.partial(gu_kernel, names=tuple(scratch)), out_sh...  178 us
    all_gather x6, waiting for transfers between devices, fetched(): return [lax.all_gather(w[number], 's', axis=0, tiled=True) for w in weights]  166 us
    pallas_call x2, Pallas kernels, down_grads(): pl.pallas_call(functools.partial(down_kernel, names=tuple(scratch)), out_...  154 us
    dot_general x5, matrix products, matmul(): return jnp.dot(a, w, preferred_element_type=f32).astype(bf16)  147 us
    dot_general x4, matrix products, step(): jnp.dot(a, w, preferred_element_type=f32)  131 us
    convert_element_type x3, other arithmetic, adamw(): return ((w - 0.02 * step).astype(bf16), m, v)  24.1 us
    psum x1, blocking collectives, step(): squares = lax.psum(sum((jnp.sum(g * g) for g in gradients)), 's')  18.5 us
  transfers between devices with their start and end apart: 6, of which 6 were waited for; matrix products, arithmetic and copies ran while one was open for 18% of the time, Pallas kernels for 0%

profile of v1, /device:TPU:1, one launch (start us, length us, event | category | flops | bytes accessed | tf_op | source)
XLA Modules:
  0.0 916.4 jit_solution(8862208460083939466)
XLA Ops:
  26.4 8.1 copy.31
  34.5 32.6 %all-gather.15.cloned.1.call-done = bf16[1,1280,3584]{2,1,0:T(8,128)(2,1)} async-done(((bf16[1,160,3584]{2,1,0:T(8,128)(2,1)}), bf16[1,1280,3584]{2,1,0:T(8,128)(2,1)}) %all-gather.15.cloned.1.call-update) | async-done | bytes 9175056 | tf_op jit(solution)/shard_map/all_gather | solution.py:453
  67.1 27.1 %fusion.28 = f32[2048,3584]{1,0:T(8,128)} fusion(bf16[1,1280,3584]{2,1,0:T(8,128)(2,1)} %all-gather.15.cloned.1.call-done, bf16[1,2048,1280]{2,1,0:T(8,128)(2,1)} %param.11, f32[2048]{0:T(1024)S(1)} %add_rsqrt_fusion.1), kind=kOutput, calls=%fused_computation.45 | convolution fusion | flops 18798346240 | bytes 43786240 | tf_op jit(solution)/shard_map/dot_general | solution.py:462
  94.2 28.3 %all-gather.17.cloned.1.call-done = bf16[1,1280,3584]{2,1,0:T(8,128)(2,1)} async-done(((bf16[1,160,3584]{2,1,0:T(8,128)(2,1)}), bf16[1,1280,3584]{2,1,0:T(8,128)(2,1)}) %all-gather.17.cloned.1.call-update) | async-done | bytes 9175056 | tf_op jit(solution)/shard_map/all_gather | solution.py:453
  122.5 35.5 %multiply_convert_fusion.1 = (bf16[2048,3584]{1,0:T(8,128)(2,1)}, f32[2048,3584]{1,0:T(8,128)}) fusion(f32[2048,3584]{1,0:T(8,128)} %fusion.28, bf16[1,1280,3584]{2,1,0:T(8,128)(2,1)} %all-gather.17.cloned.1.call-done, bf16[1,2048,1280]{2,1,0:T(8,128)(2,1)} %param.11, f32[2048]{0:T(1024)S(1)} %add_rsqrt_fusion.1), kind=kOutput, calls=%fused_computation.13 | convolution fusion | flops 18842386432 | bytes 87826432 | tf_op jit(solution)/shard_map/dot_general | solution.py:462
  158.0 19.9 %all-gather.19.cloned.1.call-done = bf16[1,3584,1280]{2,1,0:T(8,128)(2,1)} async-done(((bf16[1,448,1280]{2,1,0:T(8,128)(2,1)}), bf16[1,3584,1280]{2,1,0:T(8,128)(2,1)}) %all-gather.19.cloned.1.call-update) | async-done | bytes 9175056 | tf_op jit(solution)/shard_map/all_gather | solution.py:453
  177.9 26.2 %fusion.12 = (f32[2048]{0:T(1024)S(1)}, bf16[2048,1280]{1,0:T(8,128)(2,1)}) fusion(bf16[2048,3584]{1,0:T(8,128)(2,1)} %get-tuple-element.35.hid, bf16[1,3584,1280]{2,1,0:T(8,128)(2,1)} %all-gather.19.cloned.1.call-done, bf16[1,2048,1280]{2,1,0:T(8,128)(2,1)} %param.11), kind=kOutput, calls=%fused_computation.29 | convolution fusion | flops 18803587072 | bytes 34349056 | tf_op jit(solution)/shard_map/dot_general | solution.py:421
  204.7 28.5 %all-gather.13.cloned.1.call-done = bf16[1,3584,1280]{2,1,0:T(8,128)(2,1)} async-done(((bf16[1,448,1280]{2,1,0:T(8,128)(2,1)}), bf16[1,3584,1280]{2,1,0:T(8,128)(2,1)}) %all-gather.13.cloned.1.call-update) | async-done | bytes 9175056 | tf_op jit(solution)/shard_map/all_gather | solution.py:453
  233.2 26.3 %convolution_convert_fusion.1 = bf16[2048,3584]{1,0:T(8,128)(2,1)} fusion(bf16[1,3584,1280]{2,1,0:T(8,128)(2,1)} %all-gather.13.cloned.1.call-done, bf16[1,2048,1280]{2,1,0:T(8,128)(2,1)} %param.12), kind=kOutput, calls=%fused_computation.21 | convolution fusion | flops 18797821952 | bytes 29097984 | tf_op jit(solution)/shard_map/dot_general | solution.py:421
  259.4 29.0 %all-gather.23.cloned.1.call-done = bf16[1,1280,3584]{2,1,0:T(8,128)(2,1)} async-done(((bf16[1,160,3584]{2,1,0:T(8,128)(2,1)}), bf16[1,1280,3584]{2,1,0:T(8,128)(2,1)}) %all-gather.23.cloned.1.call-update) | async-done | bytes 9175056 | tf_op jit(solution)/shard_map/all_gather | solution.py:453
  288.4 27.1 %fusion.17 = f32[2048,3584]{1,0:T(8,128)} fusion(bf16[1,1280,3584]{2,1,0:T(8,128)(2,1)} %all-gather.23.cloned.1.call-done, bf16[2048,1280]{1,0:T(8,128)(2,1)} %get-tuple-element.38, f32[2048]{0:T(1024)S(1)} %add_rsqrt_fusion), kind=kOutput, calls=%fused_computation.34 | convolution fusion | flops 18798346240 | bytes 43786240 | tf_op jit(solution)/shard_map/dot_general | solution.py:462
  315.5 28.1 %all-gather.21.cloned.1.call-done = bf16[1,1280,3584]{2,1,0:T(8,128)(2,1)} async-done(((bf16[1,160,3584]{2,1,0:T(8,128)(2,1)}), bf16[1,1280,3584]{2,1,0:T(8,128)(2,1)}) %all-gather.21.cloned.1.call-update) | async-done | bytes 9175056 | tf_op jit(solution)/shard_map/all_gather | solution.py:453
  343.6 41.5 %multiply_convert_fusion = (bf16[2048,3584]{1,0:T(8,128)(2,1)}, bf16[2048,3584]{1,0:T(8,128)(2,1)}, bf16[2048,3584]{1,0:T(8,128)(2,1)}) fusion(f32[2048,3584]{1,0:T(8,128)} %fusion.17, bf16[2048,3584]{1,0:T(8,128)(2,1)} %convolution_convert_fusion.1, bf16[1,1280,3584]{2,1,0:T(8,128)(2,1)} %all-gather.21.cloned.1.call-done, ...), kind=kOutput, calls=%fused_computation.10 | convolution fusion | flops 18915786752 | bytes 102506496 | tf_op jit(solution)/shard_map/dot_general | solution.py:462
  385.2 26.1 %fusion.34 = bf16[2048,1280]{1,0:T(8,128)(2,1)} fusion(bf16[2048,3584]{1,0:T(8,128)(2,1)} %get-tuple-element.20.du, bf16[1,1280,3584]{2,1,0:T(8,128)(2,1)} %all-gather.21.cloned.1.call-done), kind=kOutput, calls=%fused_computation.49 | convolution fusion | flops 18793103360 | bytes 29097984 | tf_op jit(solution)/shard_map/dot_general | solution.py:421
  411.3 26.1 %fusion.40 = bf16[2048,1280]{1,0:T(8,128)(2,1)} fusion(bf16[2048,1280]{1,0:T(8,128)(2,1)} %fusion.34, bf16[2048,3584]{1,0:T(8,128)(2,1)} %get-tuple-element.19.dg, bf16[1,1280,3584]{2,1,0:T(8,128)(2,1)} %all-gather.23.cloned.1.call-done), kind=kOutput, calls=%fused_computation.54 | convolution fusion | flops 18795724800 | bytes 34340864 | tf_op jit(solution)/shard_map/dot_general | solution.py:421
  451.6 75.5 %down_grads.2 = bf16[1,4,4,56,640]{4,3,2,1,0:T(8,128)(2,1)} custom-call(bf16[2048,3584]{1,0:T(8,128)(2,1)} %get-tuple-element.35.hid, bf16[2048,1280]{1,0:T(8,128)(2,1)} %fusion.49.dy), custom_call_target="tpu_custom_call" | custom-call | tf_op jit(solution)/shard_map/down_grads/pallas_call | solution.py:407
  530.7 78.1 %down_grads.3 = bf16[1,4,4,56,640]{4,3,2,1,0:T(8,128)(2,1)} custom-call(bf16[2048,3584]{1,0:T(8,128)(2,1)} %get-tuple-element.18.hid, bf16[2048,1280]{1,0:T(8,128)(2,1)} %bitcast.81), custom_call_target="tpu_custom_call" | custom-call | tf_op jit(solution)/shard_map/down_grads/pallas_call | solution.py:407
  612.6 42.0 %fusion.5 = (bf16[2048,3584]{1,0:T(8,128)(2,1)}, bf16[2048,3584]{1,0:T(8,128)(2,1)}) fusion(f32[2048,3584]{1,0:T(8,128)} %fusion.28, f32[2048,3584]{1,0:T(8,128)} %get-tuple-element.36, bf16[2048,1280]{1,0:T(8,128)(2,1)} %fusion.49.dy, bf16[1,3584,1280]{2,1,0:T(8,128)(2,1)} %all-gather.19.cloned.1.call-done), kind=kOutput, calls=%fused_computation.9 | convolution fusion | flops 18900582400 | bytes 102498304 | tf_op jit(solution)/shard_map/dot_general | solution.py:421
  654.6 89.9 %gu_grads.2 = bf16[7,4,4,80,128]{4,3,2,1,0:T(8,128)(2,1)} custom-call(bf16[4,2,160,2048]{3,2,1,0:T(8,128)(2,1)} %bitcast.79, bf16[2048,3584]{1,0:T(8,128)(2,1)} %get-tuple-element.22.dg, bf16[2048,3584]{1,0:T(8,128)(2,1)} %get-tuple-element.21.du), custom_call_target="tpu_custom_call" | custom-call | tf_op jit(solution)/shard_map/gu_grads/pallas_call | solution.py:299
  750.3 7.9 copy.36
  758.2 88.5 %gu_grads.3 = bf16[7,4,4,80,128]{4,3,2,1,0:T(8,128)(2,1)} custom-call(bf16[4,2,160,2048]{3,2,1,0:T(8,128)(2,1)} %bitcast.80, bf16[2048,3584]{1,0:T(8,128)(2,1)} %get-tuple-element.19.dg, bf16[2048,3584]{1,0:T(8,128)(2,1)} %get-tuple-element.20.du), custom_call_target="tpu_custom_call" | custom-call | tf_op jit(solution)/shard_map/gu_grads/pallas_call | solution.py:299
  865.5 18.5 %psum.7 = f32[]{:T(128)} all-reduce(f32[]{:T(128)S(6)} %add.103), channel_id=1, replica_groups=mesh['rep'=1,'r'=16,'s'=8] {'s'}, use_global_device_ids=true, to_apply=%region_6.7 | all-reduce | flops 1 | bytes 8 | tf_op jit(solution)/shard_map/psum | solution.py:480
  884.8 9.8 %fusion.64 = (bf16[2,448,1280]{2,1,0:T(8,128)(2,1)}, f32[2,448,1280]{2,1,0:T(8,128)}, f32[2,448,1280]{2,1,0:T(8,128)}) fusion(bf16[2,448,1280]{2,1,0:T(8,128)(2,1)} %param.15, f32[]{:T(128)S(6)} %min.3, bf16[1,448,1280]{2,1,0:T(8,128)(2,1)S(1)} %copy-done.1, bf16[1,448,1280]{2,1,0:T(8,128)(2,1)S(1)} %copy-done, f32[2,448,1280]{2,1,0:T(8,128)} %param.21, ...), kind=kLoop, calls=%fused_computation.86 | loop fusion | flops 22937600 | bytes 25231364 | tf_op jit(solution)/shard_map/convert_element_type | solution.py:437
  894.6 8.8 fusion.61
  (81 shorter events, 69.6 us)
Async XLA Ops:
  7.2 6.6 copy-start.6
  7.2 59.9 %all-gather.15.cloned.1.call-start = ((), (), s32[]{:S(2)}) async-start(), calls=%async_computation.1 | async-start | bytes 10321920 | tf_op jit(solution)/shard_map/all_gather | solution.py:453
  10.5 112.0 %all-gather.17.cloned.1.call-start = ((), (), s32[]{:S(2)}) async-start(), calls=%async_computation.2 | async-start | bytes 10321920 | tf_op jit(solution)/shard_map/all_gather | solution.py:453
  13.8 164.2 %all-gather.19.cloned.1.call-start = ((), (), s32[]{:S(2)}) async-start(), calls=%async_computation.3 | async-start | bytes 10321920 | tf_op jit(solution)/shard_map/all_gather | solution.py:453
  15.4 217.8 %all-gather.13.cloned.1.call-start = ((), (), s32[]{:S(2)}) async-start(), calls=%async_computation | async-start | bytes 10321920 | tf_op jit(solution)/shard_map/all_gather | solution.py:453
  15.9 272.4 %all-gather.23.cloned.1.call-start = ((), (), s32[]{:S(2)}) async-start(), calls=%async_computation.5 | async-start | bytes 10321920 | tf_op jit(solution)/shard_map/all_gather | solution.py:453
  16.5 327.1 %all-gather.21.cloned.1.call-start = ((), (), s32[]{:S(2)}) async-start(), calls=%async_computation.4 | async-start | bytes 10321920 | tf_op jit(solution)/shard_map/all_gather | solution.py:453
  385.2 52.2 %slice-start.2 = ((s8[5242880]{0:T(1024)(128)(4,1)}), s8[4194304]{0:T(1024)(128)(4,1)S(1)}, s32[]{:S(2)}) async-start(s8[5242880]{0:T(1024)(128)(4,1)} %bitcast.84), calls=%async_computation.8 | async-start | bytes 8388608
  385.2 59.3 %slice-start = ((s8[5242880]{0:T(1024)(128)(4,1)}), s8[4194304]{0:T(1024)(128)(4,1)S(1)}, s32[]{:S(2)}) async-start(s8[5242880]{0:T(1024)(128)(4,1)} %bitcast.82), calls=%async_computation.6 | async-start | bytes 8388608
  411.3 26.1 %slice-start.3 = ((s8[5242880]{0:T(1024)(128)(4,1)}), s8[1048576]{0:T(1024)(128)(4,1)S(1)}, s32[]{:S(2)}) async-start(s8[5242880]{0:T(1024)(128)(4,1)} %bitcast.84), calls=%async_computation.9 | async-start | bytes 2097152
  411.3 33.2 %slice-start.1 = ((s8[5242880]{0:T(1024)(128)(4,1)}), s8[1048576]{0:T(1024)(128)(4,1)S(1)}, s32[]{:S(2)}) async-start(s8[5242880]{0:T(1024)(128)(4,1)} %bitcast.82), calls=%async_computation.7 | async-start | bytes 2097152
  437.4 7.0 copy-start.10
  849.5 9.1 copy-start
  849.5 9.1 copy-start.1
  849.5 10.9 %copy-start.2 = (bf16[1,160,3584]{2,1,0:T(8,128)(2,1)S(1)}, bf16[1,160,3584]{2,1,0:T(8,128)(2,1)}, u32[]{:S(2)}) copy-start(bf16[1,160,3584]{2,1,0:T(8,128)(2,1)} %slice.49) | copy-start | bytes 3440644
  884.7 9.8 %copy-start.3 = (bf16[1,160,3584]{2,1,0:T(8,128)(2,1)S(1)}, bf16[1,160,3584]{2,1,0:T(8,128)(2,1)}, u32[]{:S(2)}) copy-start(bf16[1,160,3584]{2,1,0:T(8,128)(2,1)} %slice.53) | copy-start | bytes 3440644
  884.7 9.8 %copy-start.5 = (bf16[1,160,3584]{2,1,0:T(8,128)(2,1)S(1)}, bf16[1,160,3584]{2,1,0:T(8,128)(2,1)}, u32[]{:S(2)}) copy-start(bf16[1,160,3584]{2,1,0:T(8,128)(2,1)} %slice.55) | copy-start | bytes 3440644
  884.7 9.8 %copy-start.7 = (bf16[2,160,3584]{2,1,0:T(8,128)(2,1)S(1)}, bf16[2,160,3584]{2,1,0:T(8,128)(2,1)}, u32[]{:S(2)}) copy-start(bf16[2,160,3584]{2,1,0:T(8,128)(2,1)} %param.14) | copy-start | bytes 6881284
  884.7 18.6 %slice-start.4 = ((s8[4587520]{0:T(1024)(128)(4,1)}), s8[4194304]{0:T(1024)(128)(4,1)S(1)}, s32[]{:S(2)}) async-start(s8[4587520]{0:T(1024)(128)(4,1)} %bitcast.90), calls=%async_computation.10 | async-start | bytes 8388608
  884.8 18.6 %slice-start.6 = ((s8[4587520]{0:T(1024)(128)(4,1)}), s8[4194304]{0:T(1024)(128)(4,1)S(1)}, s32[]{:S(2)}) async-start(s8[4587520]{0:T(1024)(128)(4,1)} %bitcast.92), calls=%async_computation.12 | async-start | bytes 8388608
  894.6 8.8 copy-start.4
  894.6 8.8 copy-start.8
  894.6 8.8 slice-start.5
  894.6 8.8 slice-start.7
  (1 other events, 0.6 us)
Sparse Core Ops, SparseCore 0:
  10.7 56.3 all-gather.14
  69.4 53.0 all-gather.16
  124.8 53.0 all-gather.18
  180.0 53.0 all-gather.12
  235.3 53.0 all-gather.22
  290.5 53.0 all-gather.20

commit v2 on v0

v2 whole, which is shorter than its diff:
```python
import functools

import jax
import jax.numpy as jnp
from jax import lax
from jax.experimental import pallas as pl
from jax.experimental.pallas import tpu as pltpu
from jax.sharding import PartitionSpec as P

bf16, f32 = jnp.bfloat16, jnp.float32
MESH = pl.DeviceIdType.MESH
VMEM_ALL = 67043328
T, D, F, LAYERS = 2048, 1280, 3584, 2
CORES, RING, LANES = 2, 4, 128
BLOCKS = RING * CORES
N, TILE = 512, 1024
CHUNKS = F // N
ROWS, ROWS_DOWN = D // BLOCKS, F // BLOCKS
WIDE = F // RING
X, Y, Z = range(3)
AXES = (X, Y, Z)
ORDERS = ((X, Y, Z), (Y, Z, X), (Z, X, Y))
OTHERS = (1, 3, 2)
ALL = slice(None)
ROW_BY_ROW, BY_LAST = (((0,), (0,)), ((), ())), (((1,), (1,)), ((), ()))


def at(i, n):
    return pl.ds(pl.multiple_of(i * n, n), n)


def sem(*shape):
    return pltpu.SemaphoreType.DMA(shape)


def loop(n, body):
    def step(i, none):
        body(i)
        return none

    lax.fori_loop(0, n, step, 0)


def when(condition, do, *args):
    pl.when(condition)(functools.partial(do, *args))


def within(t, n, stage):
    when((t >= 0) & (t < n), stage, t)


def start(copies):
    for copy in copies:
        copy.start()


def wait(copies):
    for copy in copies:
        copy.wait()


def arrive(ref, semaphore):
    pltpu.make_async_copy(ref, ref, semaphore).wait()


def send(src, dst, sent, come, to):
    pltpu.make_async_remote_copy(src_ref=src, dst_ref=dst, send_sem=sent, recv_sem=come, device_id=to, device_id_type=MESH).start()


class Place:
    def __init__(self):
        r, s = lax.axis_index("r"), lax.axis_index("s")
        self.rep = lax.axis_index("rep")
        self.core = lax.rem(s, CORES)
        self.at = (s // CORES, r // RING, lax.rem(r, RING))

    def id(self, x, y, z, core):
        return (self.rep, y * RING + z, x * CORES + core)

    def along(self, axis, k):
        there = list(self.at)
        there[axis] = lax.rem(there[axis] + k, RING)
        return there[axis], self.id(*there, self.core)

    def partner(self):
        return self.id(*self.at, 1 - self.core)

    def shard_group(self):
        x, y, z = self.at
        return [self.id(lax.rem(x + k, RING), y, z, 1 - self.core) for k in OTHERS]

    def meet(self, more=()):
        barrier = pltpu.get_barrier_semaphore()
        ids = [self.partner()] + [self.along(a, k)[1] for a in AXES for k in OTHERS] + list(more)
        for i in ids:
            pl.semaphore_signal(barrier, device_id=i, device_id_type=MESH)
        pl.semaphore_wait(barrier, len(ids))


class Gather:
    ALONE, QUARTER = 32, 16

    @staticmethod
    def scratch():
        return dict(g_own=sem(CHUNKS), g_snd=sem(3, CHUNKS), g_rcv=sem(3, CHUNKS))

    def __init__(self, place, refs, w, sources, layer, blocks=None):
        self.place, self.w, self.sources, self.layer, self.blocks = place, w, sources, layer, blocks
        self.own, self.snd, self.rcv = refs["g_own"], refs["g_snd"], refs["g_rcv"]
        _, y, z = place.at
        self.parts = [pl.ds(pl.multiple_of(self.ALONE + self.QUARTER * i, self.QUARTER), self.QUARTER) for i in (y, RING + z)]

    def some(self, j, parts, semaphores, stage):
        arrive(self.w.at[j, :, pl.ds(0, 3), 0, pl.ds(0, parts)], semaphores.at[stage, j])

    def start_x(self, j):
        mine = self.w.at[j, :, self.place.at[X], self.place.core]
        for m, source in enumerate(self.sources):
            for k in OTHERS:
                _, to = self.place.along(X, k)
                for rows in [pl.ds(0, self.ALONE)] + self.parts:
                    send(source.at[self.layer, rows, at(j, N)], mine.at[m, rows], self.snd.at[X, j], self.rcv.at[X, j], to)
            block = source.at[self.layer] if self.blocks is None else self.blocks.at[m]
            pltpu.make_async_copy(block.at[:, at(j, N)], mine.at[m], self.own.at[j]).start()

    def start_yz(self, j):
        self.some(j, self.ALONE + 2 * self.QUARTER, self.rcv, X)
        for k in OTHERS:
            for axis, rows in zip((Y, Z), self.parts, strict=True):
                _, to = self.place.along(axis, k)
                for i in OTHERS:
                    part = self.w.at[j, :, self.place.along(X, i)[0], self.place.core, rows]
                    send(part, part, self.snd.at[Y, j], self.rcv.at[Y, j], to)

    def start_d(self, j):
        self.some(j, 2 * 3 * self.QUARTER, self.rcv, Y)
        arrive(self.w.at[j, :, 0, 0], self.own.at[j])
        half = self.w.at[j, :, :, self.place.core]
        send(half, half, self.snd.at[Z, j], self.rcv.at[Z, j], self.place.partner())

    def ready(self, j):
        arrive(self.w.at[j, :, :, 0], self.rcv.at[Z, j])

    def finish(self):
        def one(j):
            self.some(j, self.ALONE + 2 * self.QUARTER, self.snd, X)
            self.some(j, 2 * 3 * self.QUARTER, self.snd, Y)
            arrive(self.w.at[j, :, :, 0], self.snd.at[Z, j])

        loop(CHUNKS, one)


class DownGather:
    UNITS = 5
    ALONE, QUARTER = 64, 48

    @classmethod
    def scratch(cls):
        return dict(block=pltpu.VMEM((ROWS_DOWN, D), bf16), d_own=sem(2), d_snd=sem(3, cls.UNITS), d_rcv=sem(3, cls.UNITS))

    def __init__(self, place, refs, d, source, layer):
        self.place, self.d, self.source = place, d, source.at[layer]
        self.block, self.snd, self.rcv = refs["block"], refs["d_snd"], refs["d_rcv"]
        mine = d.at[place.at[X], place.core]
        self.load, self.store = (
            pltpu.make_async_copy(a, b, refs["d_own"].at[i]) for i, (a, b) in enumerate(((self.source, self.block), (self.block, mine)))
        )
        _, y, z = place.at
        self.parts = [pl.ds(pl.multiple_of(self.ALONE + self.QUARTER * i, 16), self.QUARTER) for i in (y, RING + z)]

    def columns(self, u):
        return at(u, D // self.UNITS)

    def some(self, u, parts, semaphores, stage):
        arrive(self.d.at[pl.ds(0, 3), 0, pl.ds(0, parts), pl.ds(0, D // self.UNITS)], semaphores.at[stage, u])

    def whole(self, u, semaphores):
        arrive(self.d.at[:, 0, :, pl.ds(0, D // self.UNITS)], semaphores.at[Z, u])

    def start_x(self, u):
        for k in OTHERS:
            _, to = self.place.along(X, k)
            for rows in [pl.ds(0, self.ALONE)] + self.parts:
                there = self.d.at[self.place.at[X], self.place.core, rows, self.columns(u)]
                send(self.source.at[rows, self.columns(u)], there, self.snd.at[X, u], self.rcv.at[X, u], to)

    def start_yz(self, u):
        self.some(u, self.ALONE + 2 * self.QUARTER, self.rcv, X)
        for k in OTHERS:
            for axis, rows in zip((Y, Z), self.parts, strict=True):
                _, to = self.place.along(axis, k)
                for i in OTHERS:
                    part = self.d.at[self.place.along(X, i)[0], self.place.core, rows, self.columns(u)]
                    send(part, part, self.snd.at[Y, u], self.rcv.at[Y, u], to)

    def start_d(self, u):
        self.some(u, 2 * 3 * self.QUARTER, self.rcv, Y)
        mine = self.d.at[self.place.at[X], self.place.core, :, self.columns(u)]
        pairs = [(self.source.at[:, self.columns(u)], mine)]
        for i in OTHERS:
            pairs.append((self.d.at[self.place.along(X, i)[0], self.place.core, :, self.columns(u)],) * 2)
        for src, dst in pairs:
            send(src, dst, self.snd.at[Z, u], self.rcv.at[Z, u], self.place.partner())

    def ready(self, u):
        self.whole(u, self.rcv)

    def finish(self):
        self.load.wait()
        self.store.start()
        loop(self.UNITS, self.ready)

        def one(u):
            self.some(u, self.ALONE + 2 * self.QUARTER, self.snd, X)
            self.some(u, 2 * 3 * self.QUARTER, self.snd, Y)
            self.whole(u, self.snd)

        loop(self.UNITS, one)
        self.store.wait()


class Sum:
    def __init__(self, name, units, rows, cols, cuts, owns=1):
        self.name, self.units, self.rows, self.cols, self.cuts, self.owns = name, units, rows, cols, cuts, owns

    def scratch(self):
        u, piece = self.units, (self.rows, self.cols)
        shapes = dict(s=pltpu.VMEM((u, RING, RING, RING) + piece, bf16), ga=pltpu.VMEM((u, RING, RING) + piece, bf16))
        for k, (r, c) in enumerate(self.cuts):
            part = (r.stop - r.start, c.stop - c.start)
            shapes[f"own{k}"] = pltpu.VMEM((self.owns, RING, RING) + part, f32)
            if self.owns < u:
                shapes[f"one{k}"] = pltpu.VMEM((RING, RING) + part, f32)
            shapes[f"two{k}"] = pltpu.VMEM((RING,) + part, f32)
            shapes[f"p{k}"] = pltpu.VMEM((u, 3, RING, RING) + part, bf16)
            shapes[f"q{k}"] = pltpu.VMEM((u, 3, RING) + part, bf16)
            shapes[f"r{k}"] = pltpu.VMEM((u, 3) + part, bf16)
        shapes.update(snd=sem(5, u, 3), rcv=sem(5, u, 3))
        return {self.name + key: value for key, value in shapes.items()}

    def bind(self, place, refs, s=None):
        self.place = place
        self.ref = {key[len(self.name) :]: ref for key, ref in refs.items() if key.startswith(self.name)}
        self.s, self.ga = self.ref["s"] if s is None else s, self.ref["ga"]
        return self

    def refs(self, *names):
        return [(k, [self.ref[f"{name}{k}"] for name in names]) for k in AXES]

    def ones(self, k, u):
        return self.ref[f"one{k}"] if self.owns < self.units else self.ref[f"own{k}"].at[u]

    def piece(self, k, q, *rest):
        rest = list(rest) or [ALL, ALL]
        return tuple(q if a == ORDERS[k][0] else rest.pop(0) for a in AXES)

    def sem(self, name, stage, u, k):
        return self.ref[name].at[stage, u, k]

    def pass_on(self, stage, u, k, axis, pair):
        for n in OTHERS:
            q, to = self.place.along(axis, n)
            send(*pair(q, n - 1), self.sem("snd", stage, u, k), self.sem("rcv", stage, u, k), to)

    def start1(self, u):
        for k, (p,) in self.refs("p"):
            self.pass_on(0, u, k, ORDERS[k][0], lambda q, n, k=k, p=p: (self.s.at[(u,) + self.piece(k, q) + self.cuts[k]], p.at[u, n]))

    def leading(self, k):
        return ORDERS[k][1] < ORDERS[k][2]

    def add1(self, u):
        for k, (p, q, own) in self.refs("p", "q", "own"):
            one = self.ones(k, u)
            arrive(p.at[u], self.sem("rcv", 0, u, k))

            def some(i, p=p, own=own, one=one):
                t = own[lax.rem(u, self.owns), i] + p[u, 0, i].astype(f32) + p[u, 1, i].astype(f32) + p[u, 2, i].astype(f32)
                one[i] = t
                p[u, 0, i] = t.astype(bf16)

            loop(RING, some)
            self.pass_on(1, u, k, ORDERS[k][1], lambda i, n, k=k, p=p, q=q: (p.at[(u, 0, i) if self.leading(k) else (u, 0, ALL, i)], q.at[u, n]))

    def add2(self, u):
        for k, (q, r, two) in self.refs("q", "r", "two"):
            one = self.ones(k, u)
            arrive(q.at[u], self.sem("rcv", 1, u, k))
            me = self.place.at[ORDERS[k][1]]
            for i in range(RING):
                mine = one[me, i] if self.leading(k) else one[i, me]
                t = mine + q[u, 0, i].astype(f32) + q[u, 1, i].astype(f32) + q[u, 2, i].astype(f32)
                two[i] = t
                q[u, 0, i] = t.astype(bf16)
            self.pass_on(2, u, k, ORDERS[k][2], lambda i, n, q=q, r=r: (q.at[u, 0, i], r.at[u, n]))

    def lines(self, u, k):
        _, y, z = self.place.at
        return [self.ga.at[(u, y, to) + self.cuts[k]] for to in (z, ALL)]

    def add3(self, u):
        _, y, z = self.place.at
        for k, (r, two) in self.refs("r", "two"):
            arrive(r.at[u], self.sem("rcv", 2, u, k))
            t = two[self.place.at[ORDERS[k][2]]] + r[u, 0].astype(f32) + r[u, 1].astype(f32) + r[u, 2].astype(f32)
            self.ga[(u, y, z) + self.cuts[k]] = t.astype(bf16)
            mine, _ = self.lines(u, k)
            self.pass_on(3, u, k, Z, lambda q, n, mine=mine: (mine, mine))

    def three(self, u, k, name, stage):
        at = (u, pl.ds(0, 3), 0) if stage == 3 else (u, pl.ds(0, 3), ALL)
        arrive(self.ga.at[at + self.cuts[k]], self.sem(name, stage, u, k))

    def gather(self, u):
        for k in AXES:
            self.three(u, k, "rcv", 3)
            _, line = self.lines(u, k)
            self.pass_on(4, u, k, Y, lambda q, n, line=line: (line, line))

    def gathered(self, u):
        for k in AXES:
            self.three(u, k, "rcv", 4)

    def finish(self):
        def one(u):
            for k, parts in self.refs("p", "q", "r"):
                for stage, part in enumerate(parts):
                    arrive(part.at[u], self.sem("snd", stage, u, k))
                for stage in (3, 4):
                    self.three(u, k, "snd", stage)

        loop(self.units, one)

    def stages(self, t):
        for lag, stage in enumerate((self.gathered, self.gather, self.add3, self.add2, self.add1)):
            within(t + lag - 5, self.units, stage)


def whole(n):
    return slice(0, n)


THIRDS = tuple((slice(a, b), whole(LANES)) for a, b in ((0, 32), (32, 48), (48, 80)))
DOWN = Sum("low_", 1, 56, D // 2, tuple((whole(56), slice(a, b)) for a, b in ((0, 256), (256, 384), (384, 640))))


def gate_up_sum(name, units, owns=1):
    return Sum(name, units, ROWS // 2, LANES, THIRDS, owns)


class GateUp:
    @staticmethod
    def scratch():
        pieces = (RING, RING, RING, ROWS // 2, LANES)
        return dict(t=pltpu.VMEM((RING, CORES, ROWS, N), f32), oh=pltpu.VMEM(pieces, f32), sb=pltpu.VMEM(pieces, bf16), halfsem=sem())

    def __init__(self, place, refs, s, come):
        self.place, self.s, self.come = place, s, come
        self.t, self.oh, self.sb, self.sent = refs["t"], refs["oh"], refs["sb"], refs["halfsem"]

    def multiply(self, u, a, sides, free=None):
        for m, side in enumerate(sides):
            self.t[...] = lax.dot_general(a[...], side[...], ROW_BY_ROW, preferred_element_type=f32).reshape(self.t.shape)
            if not m:
                when(u > 0, arrive, self.sb, self.sent)
                if free:
                    free()

            def halve(x, m=m):
                for y in range(RING):
                    for h in range(2):
                        part = (slice(h * ROWS // 2, (h + 1) * ROWS // 2), slice(y * LANES, (y + 1) * LANES))
                        self.sb[x, y, 2 * m + h] = self.t[(x, 1 - self.place.core) + part].astype(bf16)
                        self.oh[x, y, 2 * m + h] = self.t[(x, self.place.core) + part]

            loop(RING, halve)
        send(self.sb, self.s.at[u], self.sent, self.come.at[u], self.place.partner())

    def join(self, u):
        arrive(self.s.at[u], self.come.at[u])

        def one(x):
            for y in range(RING):
                for z in range(RING):
                    t = self.oh[x, y, z] + self.s[u, x, y, z].astype(f32)
                    self.oh[x, y, z] = t
                    self.s[u, x, y, z] = t.astype(bf16)

        loop(RING, one)

    def keep(self, total, u):
        for k, (own,) in total.refs("own"):
            me = self.place.at[ORDERS[k][0]]

            def some(i, k=k, own=own, me=me):
                own[lax.rem(u, total.owns), i] = self.oh[total.piece(k, me, i, ALL) + total.cuts[k]]

            loop(RING, some)

    def finish(self):
        arrive(self.sb, self.sent)


class Down:
    PIECE = (RING, RING, DOWN.rows, DOWN.cols)

    @classmethod
    def scratch(cls):
        return dict(
            hid=pltpu.VMEM((2, T, WIDE), bf16),
            td=pltpu.VMEM((CORES, ROWS_DOWN, D), f32),
            ohd=pltpu.VMEM((2,) + cls.PIECE, f32),
            sbd=pltpu.VMEM((2,) + cls.PIECE, bf16),
            hidsem=sem(2),
            f_snd=sem(2),
        )

    def __init__(self, place, total, refs, hid, come):
        self.place, self.total, self.source, self.come = place, total, hid, come
        self.hid, self.t, self.oh, self.sb, self.sem, self.sent = (refs[n] for n in ("hid", "td", "ohd", "sbd", "hidsem", "f_snd"))

    def block(self, i):
        return self.place.along(X, i + 1)[0]

    def load(self, i):
        slot = lax.rem(i, 2)
        return pltpu.make_async_copy(self.source.at[:, at(self.block(i), WIDE)], self.hid.at[slot], self.sem.at[slot])

    def multiply(self, i, dy):
        slot = lax.rem(i, 2)
        self.load(i).wait()
        when(i + 1 < RING, lambda: self.load(i + 1).start())
        self.t[...] = lax.dot_general(self.hid[slot], dy[...], ROW_BY_ROW, preferred_element_type=f32).reshape(self.t.shape)
        when(i > 1, arrive, self.sb.at[slot], self.sent.at[slot])
        for y in range(RING):
            for z in range(RING):
                row, col = (2 * y + z // 2) * DOWN.rows, (z % 2) * DOWN.cols
                part = (slice(row, row + DOWN.rows), slice(col, col + DOWN.cols))
                self.sb[slot, y, z] = self.t[(1 - self.place.core,) + part].astype(bf16)
                self.oh[slot, y, z] = self.t[(self.place.core,) + part]
        send(self.sb.at[slot], self.total.s.at[0, self.block(i)], self.sent.at[slot], self.come.at[i], self.place.partner())

    def join(self, i):
        slot, x = lax.rem(i, 2), self.block(i)
        s = self.total.s.at[0, x]
        arrive(s, self.come.at[i])

        def one(y):
            for z in range(RING):
                t = self.oh[slot, y, z] + s[y, z].astype(f32)
                self.oh[slot, y, z] = t
                s[y, z] = t.astype(bf16)

        loop(RING, one)
        (_, (p0, first)), (_, (p1, second)), (_, (p2, third)) = self.total.refs("p", "own")
        me, (cut_x, cut_y, cut_z) = self.place.at, self.total.cuts

        def pass_on(k, n, q, to):
            src, dst = ((s.at[(q, ALL) + cut_y], p1.at[0, n, x]), (s.at[(ALL, q) + cut_z], p2.at[0, n, x]))[k - 1]
            send(src, dst, self.total.sem("snd", 0, 0, k), self.total.sem("rcv", 0, 0, k), to)

        for n in OTHERS:
            for k in (1, 2):
                pass_on(k, n - 1, *self.place.along(ORDERS[k][0], n))

        def to_its_chip():
            _, to = self.place.along(X, i + 1)
            send(s.at[(ALL, ALL) + cut_x], p0.at[0, i], self.total.sem("snd", 0, 0, 0), self.total.sem("rcv", 0, 0, 0), to)

        def mine():
            for y in range(RING):
                first[0, y] = self.oh[(slot, y, ALL) + cut_x]

        when(i < RING - 1, to_its_chip)
        when(i == RING - 1, mine)
        for y in range(RING):
            second[0, x, y] = self.oh[(slot, me[Y], y) + cut_y]
            third[0, x, y] = self.oh[(slot, y, me[Z]) + cut_z]

    def run(self, dy, beside=lambda i: None):
        def step(i):
            beside(i)
            within(i, RING, lambda i: self.multiply(i, dy))
            within(i - 1, RING, self.join)

        loop(RING + 1, step)
        for slot in range(2):
            arrive(self.sb.at[slot], self.sent.at[slot])


def normed(h):
    wide = h.astype(f32)
    return (wide * lax.rsqrt(jnp.mean(wide * wide, -1, keepdims=True) + 1e-6)).astype(bf16)


def backward(by, g, u):
    by = by.astype(bf16).astype(f32)
    s = jax.nn.sigmoid(g)
    gated = g * s
    return (by * u * (s * (1.0 + g * (1.0 - s)))).astype(bf16), (by * gated).astype(bf16), (gated * u).astype(bf16)


def call(kernel, name, outs, scratch, collective_id, *args):
    anywhere = pl.BlockSpec(memory_space=pl.ANY)
    return pl.pallas_call(
        functools.partial(kernel, names=tuple(scratch)),
        out_shape=outs,
        in_specs=[anywhere] * len(args),
        out_specs=[anywhere] * len(outs),
        scratch_shapes=list(scratch.values()),
        compiler_params=pltpu.CompilerParams(collective_id=collective_id, has_side_effects=True, vmem_limit_bytes=VMEM_ALL),
        name=name,
    )(*args)


def shape(*dims, dtype=bf16):
    return jax.ShapeDtypeStruct(dims, dtype)


def named(names, scratch):
    return dict(zip(names, scratch, strict=True))


GATHERED = (CHUNKS, 2, RING, CORES, ROWS, N)


def first_kernel(x, w_gate, w_up, w_down, a_out, hid_out, gu_out, d_out, *scratch, names):
    refs = named(names, scratch)
    a, hs, gs, xsem, asem, hsem, gsem = (refs[n] for n in ("a", "hs", "gs", "xsem", "asem", "hsem", "gsem"))
    load = pltpu.make_async_copy(x, a, xsem)
    load.start()
    place = Place()
    place.meet()
    gather = Gather(place, refs, refs["w"], (w_gate, w_up), 0)
    down = DownGather(place, refs, d_out, w_down, 0)
    for j in range(3):
        gather.start_x(j)
    down.load.start()
    load.wait()

    def norm(i):
        a[at(i, 64)] = normed(a[at(i, 64)])

    loop(T // 64, norm)
    keep = pltpu.make_async_copy(a, a_out, asem)
    keep.start()

    def outs(j, i):
        return (
            pltpu.make_async_copy(hs.at[i], hid_out.at[at(i, TILE), at(j, N)], hsem.at[i]),
            pltpu.make_async_copy(gs.at[i], gu_out.at[j, :, at(i, TILE)], gsem.at[i]),
        )

    def compute(j):
        gather.ready(j)

        def tile(i):
            when(j > 0, lambda: wait(outs(j, i)))
            g, u = (jnp.dot(a[at(i, TILE)], gather.w[j, m].reshape(D, N), preferred_element_type=f32) for m in range(2))
            gs[i, 0], gs[i, 1] = g, u
            hs[i] = (g * jax.nn.sigmoid(g) * u).astype(bf16)
            start(outs(j, i))

        loop(T // TILE, tile)

    def step(t):
        within(t, CHUNKS, gather.start_yz)
        within(t + 3, CHUNKS, gather.start_x)
        within(t - 1, CHUNKS, gather.start_d)
        for stage, lag in ((down.start_x, 4), (down.start_yz, 6), (down.start_d, 7)):
            within(t - lag, down.UNITS, stage)
        within(t - 2, CHUNKS, compute)

    loop(CHUNKS + down.UNITS, step)
    down.finish()
    gather.finish()
    keep.wait()
    for i in range(T // TILE):
        wait(outs(CHUNKS - 1, i))


def first(x, w_gate, w_up, w_down, collective_id):
    scratch = dict(
        Gather.scratch(),
        **DownGather.scratch(),
        w=pltpu.VMEM(GATHERED, bf16),
        a=pltpu.VMEM((T, D), bf16),
        hs=pltpu.VMEM((T // TILE, TILE, N), bf16),
        gs=pltpu.VMEM((T // TILE, 2, TILE, N), f32),
        xsem=sem(),
        asem=sem(),
        hsem=sem(2),
        gsem=sem(2),
    )
    outs = (shape(T, D), shape(T, F), shape(CHUNKS, 2, T, N, dtype=f32), shape(RING, CORES, ROWS_DOWN, D))
    return call(first_kernel, "first", outs, scratch, collective_id, x, w_gate, w_up, w_down)


SHORT = 512


def second_kernel(x, hid, d, w_down, h_out, a_out, d1_out, *scratch, names):
    refs = named(names, scratch)
    dv, hv, xv, ho, ao, dsem, hsem, xsem, osem = (refs[n] for n in ("dv", "hv", "xv", "ho", "ao", "dsem", "hsem", "xsem", "osem"))

    def loads(i, slot):
        return (
            pltpu.make_async_copy(hid.at[at(i, SHORT)], hv.at[slot], hsem.at[slot]),
            pltpu.make_async_copy(x.at[at(i, SHORT)], xv.at[slot], xsem.at[slot]),
        )

    def stores(i, slot):
        pairs = ((ho, h_out), (ao, a_out))
        return [pltpu.make_async_copy(v.at[slot], out.at[at(i, SHORT)], osem.at[n, slot]) for n, (v, out) in enumerate(pairs)]

    load = pltpu.make_async_copy(d, dv, dsem)
    load.start()
    start(loads(0, 0))
    place = Place()
    place.meet()
    down = DownGather(place, refs, d1_out, w_down, 1)
    down.load.start()
    loop(down.UNITS, down.start_x)
    load.wait()

    def compute(i):
        slot = lax.rem(i, 2)
        wait(loads(i, slot))
        when(i + 1 < T // SHORT, lambda: start(loads(i + 1, 1 - slot)))
        when(i > 1, lambda: wait(stores(i, slot)))
        h = xv[slot] + jnp.dot(hv[slot], dv[...].reshape(F, D), preferred_element_type=f32).astype(bf16)
        ho[slot] = h
        ao[slot] = normed(h)
        start(stores(i, slot))

    def step(t):
        within(t, T // SHORT, compute)
        within(t, down.UNITS, down.start_yz)
        within(t - 1, down.UNITS, down.start_d)

    loop(down.UNITS + 1, step)
    down.finish()
    for slot in range(2):
        wait(stores(0, slot))


def second(x, hid, d, w_down, collective_id):
    pair = pltpu.VMEM((2, SHORT, D), bf16)
    scratch = dict(
        DownGather.scratch(),
        dv=pltpu.VMEM((RING, CORES, ROWS_DOWN, D), bf16),
        hv=pltpu.VMEM((2, SHORT, F), bf16),
        xv=pair,
        ho=pair,
        ao=pair,
        dsem=sem(),
        hsem=sem(2),
        xsem=sem(2),
        osem=sem(2, 2),
    )
    outs = (shape(T, D), shape(T, D), shape(RING, CORES, ROWS_DOWN, D))
    return call(second_kernel, "second", outs, scratch, collective_id, x, hid, d, w_down)


EARLY = gate_up_sum("e_", 3)
LATE = gate_up_sum("l_", CHUNKS - EARLY.units, CHUNKS - EARLY.units)


def third_kernel(a_in, dy_in, d, w_gate, w_up, hid_out, dg_out, du_out, w_out, ga_out, s_out, oh_out, *scratch, names):
    refs = named(names, scratch)
    a, dy, dv, wv, side, lsem, dsem, vsem, osem, ksem = (refs[n] for n in ("a", "dy", "dv", "wv", "side", "lsem", "dsem", "vsem", "osem", "ksem"))
    blocks = refs["blocks"]
    pairs = ((w_gate.at[1], blocks.at[0]), (w_up.at[1], blocks.at[1]), (a_in, a), (dy_in, dy))
    loads = [pltpu.make_async_copy(*pair, lsem.at[n]) for n, pair in enumerate(pairs)]
    start(loads)

    def operands(j):
        slot = lax.rem(j, 2)
        return (
            pltpu.make_async_copy(d.at[at(j, N)], dv.at[slot], dsem.at[slot]),
            pltpu.make_async_copy(w_out.at[j], wv.at[slot], vsem.at[slot]),
        )

    place = Place()
    place.meet()
    gather = Gather(place, refs, w_out, (w_gate, w_up), 1, blocks)
    wait(loads[:2])
    s = refs["s"]
    total = EARLY.bind(place, refs, s)
    grads = GateUp(place, refs, s, refs["come"])
    for j in range(3):
        gather.start_x(j)
    wait(loads[2:])

    def fetch(j):
        gather.ready(j)
        start(operands(j))

    def outs(j):
        return [pltpu.make_async_copy(side.at[n], out.at[:, at(j, N)], osem.at[n]) for n, out in enumerate((dg_out, du_out, hid_out))]

    def leave(u):
        late = u - EARLY.units
        return (pltpu.make_async_copy(s.at[u], s_out.at[late], ksem.at[0]), pltpu.make_async_copy(grads.oh, oh_out.at[late], ksem.at[1]))

    def join(u):
        grads.join(u)

        def go_on():
            grads.keep(total, u)
            total.start1(u)

        when(u < EARLY.units, go_on)
        when(u >= EARLY.units, lambda: start(leave(u)))

    def compute(j):
        slot = lax.rem(j, 2)
        wait(operands(j))
        when(j > 0, lambda: wait(outs(j)))

        def tile(i):
            rows = at(i, TILE)
            g, u = (jnp.dot(a[rows], wv[slot, m].reshape(D, N), preferred_element_type=f32) for m in range(2))
            by = lax.dot_general(dy[rows], dv[slot], BY_LAST, preferred_element_type=f32)
            side[0, rows], side[1, rows], side[2, rows] = backward(by, g, u)

        loop(T // TILE, tile)
        start(outs(j))
        within(j + 1, CHUNKS, fetch)
        total.stages(j - 1)
        within(j - 1, CHUNKS, join)
        grads.multiply(j, a, (side.at[0], side.at[1]), lambda: when(j > EARLY.units, lambda: wait(leave(j - 1))))

    def step(t):
        within(t, CHUNKS, gather.start_yz)
        within(t + 3, CHUNKS, gather.start_x)
        within(t - 1, CHUNKS, gather.start_d)
        when(t == 1, fetch, 0)
        within(t - 2, CHUNKS, compute)

    loop(CHUNKS + 2, step)
    total.stages(CHUNKS - 1)
    join(CHUNKS - 1)
    total.stages(CHUNKS)
    wait(leave(CHUNKS - 1))
    grads.finish()
    gather.finish()
    total.finish()
    wait(outs(CHUNKS - 1))
    keep = pltpu.make_async_copy(total.ga, ga_out, ksem.at[0])
    keep.start()
    keep.wait()


def third(a, dy, d, w_gate, w_up, collective_id):
    pieces = (RING, RING, RING, ROWS // 2, LANES)
    early = EARLY.scratch()
    del early["e_s"]
    scratch = dict(
        Gather.scratch(),
        **GateUp.scratch(),
        **early,
        s=pltpu.VMEM((CHUNKS,) + pieces, bf16),
        come=sem(CHUNKS),
        a=pltpu.VMEM((T, D), bf16),
        dy=pltpu.VMEM((T, D), bf16),
        dv=pltpu.VMEM((2, N, D), bf16),
        wv=pltpu.VMEM((2,) + GATHERED[1:], bf16),
        side=pltpu.VMEM((3, T, N), bf16),
        blocks=pltpu.VMEM((2, ROWS, F), bf16),
        lsem=sem(4),
        dsem=sem(2),
        vsem=sem(2),
        osem=sem(3),
        ksem=sem(2),
    )
    outs = [shape(T, F)] * 3 + [shape(*GATHERED), shape(EARLY.units, RING, RING, ROWS // 2, LANES)]
    outs += [shape(LATE.units, *pieces), shape(LATE.units, *pieces, dtype=f32)]
    return call(third_kernel, "third", outs, scratch, collective_id, a, dy, d.reshape(F, D), w_gate, w_up)


def fourth_kernel(hid, dy_in, dg, du, w, h, s_in, oh_in, dh_out, ga_out, gd_out, *scratch, names):
    refs = named(names, scratch)
    dy, lsem, csem, osem = (refs[n] for n in ("dy", "lsem", "csem", "osem"))
    load = pltpu.make_async_copy(dy_in, dy, lsem)
    load.start()
    place = Place()
    late, low = LATE.bind(place, refs), DOWN.bind(place, refs)
    carried = [pltpu.make_async_copy(s_in, late.s, csem.at[3])]
    for k, (own,) in late.refs("own"):
        pieces = (ALL,) + late.piece(k, place.at[ORDERS[k][0]]) + late.cuts[k]
        carried.append(pltpu.make_async_copy(oh_in.at[pieces], own, csem.at[k]))
    start(carried)
    place.meet()
    wait(carried)

    def late_stages(t):
        late.stages(t)
        within(t, late.units, late.start1)

    late_stages(0)

    def multiply_down(**refs_down):
        down = Down(place, low, refs_down, hid, refs["come"])
        down.load(0).start()
        load.wait()
        down.run(dy)

    pl.run_scoped(multiply_down, **Down.scratch())

    def multiply_back(gv, wv, acc, hv, gsem, hsem):
        def loads(j, slot):
            yield pltpu.make_async_copy(w.at[j], wv.at[slot], gsem.at[slot, 2])
            for n, side in enumerate((dg, du)):
                yield pltpu.make_async_copy(side.at[:, at(j, N)], gv.at[slot, n], gsem.at[slot, n])

        start(loads(0, 0))

        def step(j):
            slot = lax.rem(j, 2)
            wait(loads(j, slot))
            when(j + 1 < CHUNKS, lambda: start(loads(j + 1, 1 - slot)))
            late_stages(j + 1)
            low.stages(j)

            def tile(i):
                rows = at(i, SHORT)
                by, more = (lax.dot_general(gv[slot, m, rows], wv[slot, m].reshape(D, N), BY_LAST, preferred_element_type=f32) for m in range(2))
                by += more

                def first_time():
                    acc[rows] = by

                def again():
                    acc[rows] += by

                when(j == 0, first_time)
                when(j > 0, again)

            loop(T // SHORT, tile)

        loop(CHUNKS, step)

        def tile_of_h(i):
            slot = lax.rem(i, 2)
            return pltpu.make_async_copy(h.at[at(i, 256)], hv.at[slot], hsem.at[slot])

        tile_of_h(0).start()
        late_stages(CHUNKS + 1)

        def norm(i):
            tile_of_h(i).wait()
            when(i + 1 < T // 256, lambda: tile_of_h(i + 1).start())

            def part(n):
                rows = pl.ds(pl.multiple_of(i * 256 + n * 64, 64), 64)
                wide = hv[lax.rem(i, 2), at(n, 64)].astype(f32)
                by = acc[rows].astype(bf16).astype(f32)
                scale = lax.rsqrt(jnp.mean(wide * wide, -1, keepdims=True) + 1e-6)
                along = jnp.mean(by * wide, -1, keepdims=True)
                dy[rows] = dy[rows] + (by * scale - wide * (scale * scale * scale * along)).astype(bf16)

            loop(4, part)

        loop(T // 256, norm)

    pl.run_scoped(
        multiply_back,
        pltpu.VMEM((2, 2, T, N), bf16),
        pltpu.VMEM((2,) + GATHERED[1:], bf16),
        pltpu.VMEM((T, D), f32),
        pltpu.VMEM((2, 256, D), bf16),
        sem(2, 3),
        sem(2),
    )
    results = [pltpu.make_async_copy(v, out, osem.at[n]) for n, (v, out) in enumerate(((dy, dh_out), (late.ga, ga_out), (low.ga.at[0], gd_out)))]
    start(results)
    late.finish()
    low.finish()
    wait(results)


def fourth(hid, dy, dg, du, w, h, s, oh, collective_id):
    scratch = dict(
        LATE.scratch(),
        **DOWN.scratch(),
        come=sem(RING),
        dy=pltpu.VMEM((T, D), bf16),
        lsem=sem(),
        csem=sem(4),
        osem=sem(3),
    )
    outs = [shape(T, D), shape(LATE.units, RING, RING, ROWS // 2, LANES), shape(*Down.PIECE)]
    return call(fourth_kernel, "fourth", outs, scratch, collective_id, hid, dy, dg, du, w, h, s, oh)


LAST = gate_up_sum("e_", CHUNKS)


def fifth_kernel(hid, dy_in, a_in, d, gu, ga_early, ga_late, gd_in, ga_out, gd_out, sum_out, *scratch, names):
    refs = named(names, scratch)
    dy, lsem, osem = (refs[n] for n in ("dy", "lsem", "osem"))
    load = pltpu.make_async_copy(dy_in, dy, lsem)
    load.start()
    place = Place()
    others = place.shard_group()
    place.meet(others)
    total, low = LAST.bind(place, refs), DOWN.bind(place, refs)

    def multiply_down(**refs_down):
        down = Down(place, low, refs_down, hid, refs["come"])
        down.load(0).start()
        load.wait()
        down.run(dy)

    pl.run_scoped(multiply_down, **Down.scratch())
    tiles, ahead = T // SHORT, 3

    def multiply_gates(a, dv, gv, side, asem, dsem, gsem, **refs_grads):
        grads = GateUp(place, refs_grads, total.s, refs["arrived"])
        load_a = pltpu.make_async_copy(a_in, a, asem)

        def rows_of_d(j):
            return pltpu.make_async_copy(d.at[at(j, N)], dv, dsem)

        def tile_of_gu(n):
            slot = lax.rem(n, ahead)
            return pltpu.make_async_copy(gu.at[n // tiles, :, at(lax.rem(n, tiles), SHORT)], gv.at[slot], gsem.at[slot])

        start([rows_of_d(0), load_a] + [tile_of_gu(n) for n in range(ahead)])

        def join(u):
            grads.join(u)
            grads.keep(total, u)
            total.start1(u)

        def back(j):
            rows_of_d(j).wait()

            def tile(i):
                n = j * tiles + i
                tile_of_gu(n).wait()
                by = lax.dot_general(dy[at(i, SHORT)], dv[...], BY_LAST, preferred_element_type=f32)
                side[0, at(i, SHORT)], side[1, at(i, SHORT)], _ = backward(by, gv[lax.rem(n, ahead), 0], gv[lax.rem(n, ahead), 1])
                when(n + ahead < CHUNKS * tiles, lambda: tile_of_gu(n + ahead).start())

            loop(tiles, tile)
            when(j + 1 < CHUNKS, lambda: rows_of_d(j + 1).start())

        def step(t):
            within(t, CHUNKS, back)
            low.stages(t)
            total.stages(t - 1)
            within(t - 1, CHUNKS, join)
            when(t == 0, load_a.wait)
            within(t, CHUNKS, lambda j: grads.multiply(j, a, (side.at[0], side.at[1])))

        loop(CHUNKS + 1, step)
        grads.finish()

    pl.run_scoped(
        multiply_gates,
        pltpu.VMEM((T, D), bf16),
        pltpu.VMEM((N, D), bf16),
        pltpu.VMEM((ahead, 2, SHORT, N), f32),
        pltpu.VMEM((2, T, N), bf16),
        sem(),
        sem(),
        sem(ahead),
        **GateUp.scratch(),
    )

    def square(g, d, gsem):
        loads = [pltpu.make_async_copy(*pair, gsem.at[n]) for n, pair in enumerate(((ga_early, g.at[:EARLY.units]), (ga_late, g.at[EARLY.units :]), (gd_in, d)))]
        start(loads)
        total.stages(CHUNKS)
        squares = refs["squares"]
        me = place.at[X] * CORES + place.core
        mine = squares.at[me]
        mine[...] = jnp.zeros(mine.shape, f32)

        def add(piece):
            for n in range(0, piece.shape[1], LANES):
                t = piece[:, n : n + LANES].astype(f32)
                mine[...] += jnp.sum((t * t).reshape((-1,) + mine.shape), 0)

        def add_all(all_gates, all_down):
            loop(CHUNKS * RING, lambda i: [add(all_gates[i // RING, lax.rem(i, RING), z]) for z in range(RING)])
            loop(RING, lambda y: [add(all_down[y, z]) for z in range(RING)])

        wait(loads)
        add_all(g, d)
        loop(4, lambda t: total.stages(t + CHUNKS + 1))
        add_all(total.ga, low.ga.at[0])
        for to in others + [place.partner()] + [place.along(X, k)[1] for k in OTHERS]:
            send(mine, mine, refs["q_snd"], refs["q_rcv"], to)
        for semaphore in (refs["q_rcv"], refs["q_snd"]):
            arrive(squares.at[: BLOCKS - 1], semaphore)
        sum_ref = refs["sum"]
        sum_ref[...] = squares[0]
        for n in range(1, BLOCKS):
            sum_ref[...] += squares[n]

    pl.run_scoped(square, pltpu.VMEM(total.ga.shape, bf16), pltpu.VMEM(Down.PIECE, bf16), sem(3))
    results = [pltpu.make_async_copy(v, out, osem.at[n]) for n, (v, out) in enumerate(((total.ga, ga_out), (low.ga.at[0], gd_out), (refs["sum"], sum_out)))]
    start(results)
    total.finish()
    low.finish()
    wait(results)


def fifth(hid, dy, a, d, gu, *layer1, collective_id):
    scratch = dict(
        LAST.scratch(),
        **DOWN.scratch(),
        come=sem(RING),
        arrived=sem(CHUNKS),
        dy=pltpu.VMEM((T, D), bf16),
        lsem=sem(),
        osem=sem(3),
        squares=pltpu.VMEM((BLOCKS, 8, LANES), f32),
        sum=pltpu.VMEM((8, LANES), f32),
        q_snd=sem(),
        q_rcv=sem(),
    )
    outs = [shape(CHUNKS, RING, RING, ROWS // 2, LANES), shape(*Down.PIECE), shape(8, LANES, dtype=f32)]
    return call(fifth_kernel, "fifth", outs, scratch, collective_id, hid, dy, a, d.reshape(F, D), gu, *layer1)


SLOTS = 4
TALL = 2 * 2 * DOWN.rows


def sixth_kernel(*args, names):
    (total, *gradients), args = args[:6], args[6:]
    weights, outs, refs = args[:9], args[9:18], named(names, args[18:])
    g1, g0, d1, d0, sv = (refs[n] for n in ("g1", "g0", "d1", "d0", "sv"))
    early, late, down1, both0, down0 = gradients
    pairs = ((total, sv), (early, g1.at[: EARLY.units]), (late, g1.at[EARLY.units :]), (both0, g0), (down1, d1), (down0, d0))
    loads = [pltpu.make_async_copy(*pair, refs["lsem"].at[n]) for n, pair in enumerate(pairs)]
    start(loads)

    def copies(n, arrays, into, which, kind):
        per, rows, buffers = (RING, ROWS // 2, ("gw", "gm", "gv")) if kind < 2 else (2, TALL, ("dw", "dm", "dv"))
        slot = lax.rem(n, SLOTS)
        for i, buffer in enumerate(buffers):
            there, here = arrays[3 * i + kind].at[n // per, at(lax.rem(n, 2), rows)], refs[buffer].at[slot]
            yield pltpu.make_async_copy(*((there, here) if into else (here, there)), refs["sems"].at[which, kind // 2, slot, i])

    def gates(n, do, arrays, into, which):
        for kind in range(2):
            when(lax.rem(n, RING) // 2 == kind, lambda kind=kind: do(copies(n, arrays, into, which, kind)))

    def downs(n, do, arrays, into, which):
        do(copies(n, arrays, into, which, 2))

    wait(loads[:1])
    squares = jnp.sum(sv[...], keepdims=True)
    factor = jnp.minimum(1.0, 0.5 * lax.rsqrt(squares / (LAYERS * 3 * D * F) + 1e-30))

    def adamw(slot, buffers, part, g):
        w, m, v = (refs[b].at[slot] for b in buffers)
        g = g.astype(f32) * factor
        new_m = 0.9 * m[part] + 0.1 * g
        new_v = 0.95 * v[part] + 0.05 * g * g
        old = w[part].astype(f32)
        w[part] = (old - 0.02 * (new_m * lax.rsqrt(new_v + 1e-8) + 0.1 * old)).astype(bf16)
        m[part], v[part] = new_m, new_v

    def run(steps, transfer, body):
        for n in range(SLOTS - 1):
            transfer(jnp.int32(n), start, weights, True, 0)

        def step(n):
            transfer(n, wait, weights, True, 0)
            body(n, lax.rem(n, SLOTS))
            transfer(n, start, outs, False, 1)
            when(n > 0, lambda: transfer(n - 1, wait, outs, False, 1))
            within(n + SLOTS - 1, steps, lambda n: transfer(n, start, weights, True, 0))

        loop(steps, step)
        transfer(jnp.int32(steps - 1), wait, outs, False, 1)

    def gate_step(n, slot):
        def of(g):
            for j in range(CHUNKS):
                for y in range(RING):
                    columns = slice(j * N + y * LANES, j * N + (y + 1) * LANES)
                    adamw(slot, ("gw", "gm", "gv"), (ALL, columns), g[j, y, lax.rem(n, RING)])

        when(n < RING, of, g0)
        when(n >= RING, of, g1)

    def down_step(n, slot):
        def of(d):
            for y in range(2):
                for z in range(RING):
                    row, col = (2 * y + z // 2) * DOWN.rows, (z % 2) * DOWN.cols
                    part = (slice(row, row + DOWN.rows), slice(col, col + DOWN.cols))
                    adamw(slot, ("dw", "dm", "dv"), part, d[2 * lax.rem(n, 2) + y, z])

        when(n < 2, of, d0)
        when(n >= 2, of, d1)

    wait(loads[1:])
    run(LAYERS * RING, gates, gate_step)
    run(LAYERS * 2, downs, down_step)


def sixth(total, gradients, weights):
    half, tall = (SLOTS, ROWS // 2, F), (SLOTS, TALL, D)
    pieces = pltpu.VMEM((CHUNKS, RING, RING, ROWS // 2, LANES), bf16)
    scratch = dict(g1=pieces, g0=pieces, d1=pltpu.VMEM(Down.PIECE, bf16), d0=pltpu.VMEM(Down.PIECE, bf16), sv=pltpu.VMEM((8, LANES), f32))
    for name, dims in (("g", half), ("d", tall)):
        scratch.update({name + "w": pltpu.VMEM(dims, bf16), name + "m": pltpu.VMEM(dims, f32), name + "v": pltpu.VMEM(dims, f32)})
    scratch.update(lsem=sem(6), sems=sem(2, 2, SLOTS, 3))
    outs = [shape(*w.shape, dtype=w.dtype) for w in weights]
    return call(sixth_kernel, "sixth", outs, scratch, None, total, *gradients, *weights)


def solution(mesh):
    def step(x, dy, *arrays):
        w_gate, w_up, w_down = arrays[:3]
        x, dy = x[0], dy[0]
        a0, hid0, gu0, d0 = first(x, w_gate, w_up, w_down, 0)
        h1, a1, d1 = second(x, hid0, d0, w_down, 1)
        hid1, dg1, du1, w1, early, s, oh = third(a1, dy, d1, w_gate, w_up, 2)
        dh1, late, down1 = fourth(hid1, dy, dg1, du1, w1, h1, s, oh, 3)
        both0, down0, total = fifth(hid0, dh1, a0, d0, gu0, early, late, down1, collective_id=4)
        return tuple(sixth(total, (early, late, down1, both0, down0), arrays))

    states, cut = P(("rep", "r", "s"), None, None), P(None, "s", None)
    return jax.shard_map(
        step,
        mesh=mesh,
        in_specs=(states, states) + (cut,) * 9,
        out_specs=(P("rep", "s", None),) * 9,
        check_vma=False,
    )
```

time: 1030 us -> 596 us (0.58)
  Pallas kernels: 0 us -> 589 us
  waiting for transfers between devices: 461 us -> 0 us
  matrix products: 452 us -> 0 us
  other arithmetic: 48.3 us -> 0 us
  local copies, waits for them, and re-layouts: 25.1 us -> 0 us
  between operations: 17.1 us -> 1.15 us
  blocking collectives: 13.4 us -> 0 us
    pallas_call x0 -> x6, Pallas kernels: none -> 589 us  [call(): pl.pallas_call(functools.partial(kernel, names=tuple(scratch)), out_shape...]
    dot_general x15 -> x0, matrix products: 452 us -> none  [the longest x5 160 us: layer(): gate = jnp.dot(a, w['w_gate'], preferred_element_type=jnp.float32)]
    reduce_scatter x6 -> x0, waiting for transfers between devices: 165 us -> none  [summed(): lax.psum_scatter(term, 's', scatter_dimension=0, tiled=True)]
    all_gather x6 -> x0, waiting for transfers between devices: 163 us -> none  [fetched(): lax.all_gather(w[number], 's', axis=0, tiled=True)]
    psum x1 -> x0, waiting for transfers between devices: 132 us -> none  [summed(): lax.psum(lax.psum_scatter(term, 's', scatter_dimension=0, tiled=True), 'r')]
    convert_element_type x2 -> x0, other arithmetic: 23.7 us -> none  [adamw(): return ((w - 0.02 * step).astype(jnp.bfloat16), m, v)]
    unnamed x26 -> x0, local copies, waits for them, and re-layouts: 17.1 us -> none
    psum x1 -> x0, blocking collectives: 13.4 us -> none  [step(): squares = lax.psum(sum((jnp.sum(g * g) for g in gradients)), 's')]
  transfers between devices with their start and end apart: 13 -> 0, of which waited for: 10 -> 0; matrix products, arithmetic and copies ran while one was open for 34% -> 0% of each run, Pallas kernels for 0% -> 0%
where the time goes in v2:
time: 596 us; the launch traced here: 590 us
  Pallas kernels  589 us (99%)
    pallas_call x6, Pallas kernels, call(): pl.pallas_call(functools.partial(kernel, names=tuple(scratch)), out_shape...  589 us

profile of v2, /device:TPU:1, one launch (start us, length us, event | category | flops | bytes accessed | tf_op | source)
XLA Modules:
  0.0 590.3 jit_solution(1714914091309404272)
XLA Ops:
  0.6 82.1 %first.1 = (bf16[2048,1280]{1,0:T(8,128)(2,1)}, bf16[2048,3584]{1,0:T(8,128)(2,1)}, f32[7,2,2048,512]{3,2,1,0:T(8,128)}, bf16[4,2,448,1280]{3,2,1,0:T(8,128)(2,1)}) custom-call(bf16[2048,1280]{1,0:T(8,128)(2,1)} %bitcast.5, bf16[2,160,3584]{2,1,0:T(8,128)(2,1)} %args_6_.4, bf16[2,160,3584]{2,1,0:T(8,128)(2,1)} %args_7_.4, bf16[2,448,1280]{2,1,0:T(8,128)(2,1)} %args_8_.4), custom_call_target="tpu_custom_call" | custom-call | tf_op jit(solution)/shard_map/first/pallas_call | solution.py:505
  82.7 38.0 %second.1 = (bf16[2048,1280]{1,0:T(8,128)(2,1)}, bf16[2048,1280]{1,0:T(8,128)(2,1)}, bf16[4,2,448,1280]{3,2,1,0:T(8,128)(2,1)}) custom-call(bf16[2048,1280]{1,0:T(8,128)(2,1)} %bitcast.6, bf16[2048,3584]{1,0:T(8,128)(2,1)} %get-tuple-element.29.hid, bf16[4,2,448,1280]{3,2,1,0:T(8,128)(2,1)} %get-tuple-element.30.d, bf16[2,448,1280]{2,1,0:T(8,128)(2,1)} %args_8_.4), custom_call_target="tpu_custom_call" | custom-call | tf_op jit(solution)/shard_map/second/pallas_call | solution.py:505
  120.7 144.0 %third.1 = (bf16[2048,3584]{1,0:T(8,128)(2,1)}, bf16[2048,3584]{1,0:T(8,128)(2,1)}, bf16[2048,3584]{1,0:T(8,128)(2,1)}, bf16[7,2,4,2,160,512]{5,4,3,2,1,0:T(8,12...) custom-call(bf16[2048,1280]{1,0:T(8,128)(2,1)} %get-tuple-element.31, ...), custom_call_target="tpu_custom_call" | custom-call | tf_op jit(solution)/shard_map/third/pallas_call | solution.py:505
  264.7 125.5 %fourth.1 = (bf16[2048,1280]{1,0:T(8,128)(2,1)}, bf16[4,4,4,80,128]{4,3,2,1,0:T(8,128)(2,1)}, bf16[4,4,56,640]{3,2,1,0:T(8,128)(2,1)}) custom-call(bf16[2048,3584]{1,0:T(8,128)(2,1)} %get-tuple-element.33.hid, bf16[2048,1280]{1,0:T(8,128)(2,1)} %bitcast.8, bf16[2048,3584]{1,0:T(8,128)(2,1)} %get-tuple-element.34.dg, ...), custom_call_target="tpu_custom_call" | custom-call | tf_op jit(solution)/shard_map/fourth/pallas_call | solution.py:505
  390.2 171.3 %fifth.1 = (bf16[7,4,4,80,128]{4,3,2,1,0:T(8,128)(2,1)}, bf16[4,4,56,640]{3,2,1,0:T(8,128)(2,1)}, f32[8,128]{1,0:T(8,128)}) custom-call(bf16[2048,3584]{1,0:T(8,128)(2,1)} %get-tuple-element.29.hid, bf16[2048,1280]{1,0:T(8,128)(2,1)} %get-tuple-element.40.dy_in, bf16[2048,1280]{1,0:T(8,128)(2,1)} %get-tuple-element.41.a_in, bf16[3584,1280]{1,0:T(8,128)(2,1)} %bitcast.4, ...), custom_call_target="tpu_custom_call" | custom-call | tf_op jit(solution)/shard_map/fifth/pallas_call | solution.py:505
  561.4 28.4 %sixth.1 = (bf16[2,160,3584]{2,1,0:T(8,128)(2,1)}, bf16[2,160,3584]{2,1,0:T(8,128)(2,1)}, bf16[2,448,1280]{2,1,0:T(8,128)(2,1)}, f32[2,160,3584]{2,1,0:T(8,128)}...) custom-call(f32[8,128]{1,0:T(8,128)} %get-tuple-element.46.args_0_, ...), custom_call_target="tpu_custom_call" | custom-call | tf_op jit(solution)/shard_map/sixth/pallas_call | solution.py:505

commit v3 on v2

--- a/solution.py
+++ b/solution.py
@@ -97,126 +97,100 @@
         pl.semaphore_wait(barrier, len(ids))
 
 
-class Gather:
-    ALONE, QUARTER = 32, 16
-
-    @staticmethod
-    def scratch():
-        return dict(g_own=sem(CHUNKS), g_snd=sem(3, CHUNKS), g_rcv=sem(3, CHUNKS))
-
-    def __init__(self, place, refs, w, sources, layer, blocks=None):
-        self.place, self.w, self.sources, self.layer, self.blocks = place, w, sources, layer, blocks
-        self.own, self.snd, self.rcv = refs["g_own"], refs["g_snd"], refs["g_rcv"]
+BOTH = ((1, 0), (3, 1))
+
+
+class Fetch:
+    REST, STAGES = slice(1, RING), range(4)
+
+    def __init__(self, place, refs, w, source):
+        self.place, self.w, self.source = place, w, source
+        self.own, self.snd, self.rcv = (refs[self.name + n] for n in ("own", "snd", "rcv"))
         _, y, z = place.at
-        self.parts = [pl.ds(pl.multiple_of(self.ALONE + self.QUARTER * i, self.QUARTER), self.QUARTER) for i in (y, RING + z)]
-
-    def some(self, j, parts, semaphores, stage):
-        arrive(self.w.at[j, :, pl.ds(0, 3), 0, pl.ds(0, parts)], semaphores.at[stage, j])
-
-    def start_x(self, j):
-        mine = self.w.at[j, :, self.place.at[X], self.place.core]
-        for m, source in enumerate(self.sources):
-            for k in OTHERS:
-                _, to = self.place.along(X, k)
-                for rows in [pl.ds(0, self.ALONE)] + self.parts:
-                    send(source.at[self.layer, rows, at(j, N)], mine.at[m, rows], self.snd.at[X, j], self.rcv.at[X, j], to)
-            block = source.at[self.layer] if self.blocks is None else self.blocks.at[m]
-            pltpu.make_async_copy(block.at[:, at(j, N)], mine.at[m], self.own.at[j]).start()
-
-    def start_yz(self, j):
-        self.some(j, self.ALONE + 2 * self.QUARTER, self.rcv, X)
+        self.parts = [pl.ds(pl.multiple_of(self.alone + self.quarter * i, 16), self.quarter) for i in (y, RING + z)]
+
+    @classmethod
+    def scratch(cls):
+        shape = (len(cls.STAGES), cls.units)
+        return {cls.name + "own": sem(cls.units), cls.name + "snd": sem(*shape), cls.name + "rcv": sem(*shape)}
+
+    def copy(self, stage, u, to, src, dst=None):
+        send(src, src if dst is None else dst, self.snd.at[stage, u], self.rcv.at[stage, u], to)
+
+    def came(self, stage, u, semaphores):
+        rows = self.alone + 2 * self.quarter
+        blocks, rows = ((2, rows), (1, rows), (3, 2 * 3 * self.quarter), (RING, self.all_rows))[stage]
+        arrive(self.block(u, pl.ds(0, blocks), pl.ds(0, rows)), semaphores.at[stage, u])
+
+    def along_x(self):
+        return [(k, half, rows, self.place.along(X, k)[1]) for k, half in BOTH for rows in [pl.ds(0, self.alone)] + self.parts]
+
+    def start_x(self, u):
+        for k, _, rows, to in self.along_x():
+            self.copy(0, u, to, self.mine(u, rows), self.block(u, RING - k, rows))
+        pltpu.make_async_copy(self.mine(u, ALL), self.block(u, 0, ALL), self.own.at[u]).start()
+
+    def pass_x(self, u):
+        self.came(0, u, self.rcv)
+        for k, half, rows, to in self.along_x():
+            self.copy(1, u, to, self.block(u, RING - k, rows, half), self.block(u, 2, rows, half))
+
+    def start_yz(self, u):
+        self.came(1, u, self.rcv)
         for k in OTHERS:
             for axis, rows in zip((Y, Z), self.parts, strict=True):
-                _, to = self.place.along(axis, k)
-                for i in OTHERS:
-                    part = self.w.at[j, :, self.place.along(X, i)[0], self.place.core, rows]
-                    send(part, part, self.snd.at[Y, j], self.rcv.at[Y, j], to)
-
-    def start_d(self, j):
-        self.some(j, 2 * 3 * self.QUARTER, self.rcv, Y)
-        arrive(self.w.at[j, :, 0, 0], self.own.at[j])
-        half = self.w.at[j, :, :, self.place.core]
-        send(half, half, self.snd.at[Z, j], self.rcv.at[Z, j], self.place.partner())
-
-    def ready(self, j):
-        arrive(self.w.at[j, :, :, 0], self.rcv.at[Z, j])
+                self.copy(2, u, self.place.along(axis, k)[1], self.block(u, self.REST, rows))
+
+    def start_d(self, u):
+        self.came(2, u, self.rcv)
+        arrive(self.block(u, 0, ALL), self.own.at[u])
+        self.copy(3, u, self.place.partner(), self.block(u, ALL, ALL))
+
+    def ready(self, u):
+        self.came(3, u, self.rcv)
 
     def finish(self):
-        def one(j):
-            self.some(j, self.ALONE + 2 * self.QUARTER, self.snd, X)
-            self.some(j, 2 * 3 * self.QUARTER, self.snd, Y)
-            arrive(self.w.at[j, :, :, 0], self.snd.at[Z, j])
-
-        loop(CHUNKS, one)
-
-
-class DownGather:
-    UNITS = 5
-    ALONE, QUARTER = 64, 48
-
-    @classmethod
-    def scratch(cls):
-        return dict(block=pltpu.VMEM((ROWS_DOWN, D), bf16), d_own=sem(2), d_snd=sem(3, cls.UNITS), d_rcv=sem(3, cls.UNITS))
-
-    def __init__(self, place, refs, d, source, layer):
-        self.place, self.d, self.source = place, d, source.at[layer]
-        self.block, self.snd, self.rcv = refs["block"], refs["d_snd"], refs["d_rcv"]
-        mine = d.at[place.at[X], place.core]
-        self.load, self.store = (
-            pltpu.make_async_copy(a, b, refs["d_own"].at[i]) for i, (a, b) in enumerate(((self.source, self.block), (self.block, mine)))
-        )
-        _, y, z = place.at
-        self.parts = [pl.ds(pl.multiple_of(self.ALONE + self.QUARTER * i, 16), self.QUARTER) for i in (y, RING + z)]
-
-    def columns(self, u):
-        return at(u, D // self.UNITS)
-
-    def some(self, u, parts, semaphores, stage):
-        arrive(self.d.at[pl.ds(0, 3), 0, pl.ds(0, parts), pl.ds(0, D // self.UNITS)], semaphores.at[stage, u])
-
-    def whole(self, u, semaphores):
-        arrive(self.d.at[:, 0, :, pl.ds(0, D // self.UNITS)], semaphores.at[Z, u])
-
-    def start_x(self, u):
-        for k in OTHERS:
-            _, to = self.place.along(X, k)
-            for rows in [pl.ds(0, self.ALONE)] + self.parts:
-                there = self.d.at[self.place.at[X], self.place.core, rows, self.columns(u)]
-                send(self.source.at[rows, self.columns(u)], there, self.snd.at[X, u], self.rcv.at[X, u], to)
-
-    def start_yz(self, u):
-        self.some(u, self.ALONE + 2 * self.QUARTER, self.rcv, X)
-        for k in OTHERS:
-            for axis, rows in zip((Y, Z), self.parts, strict=True):
-                _, to = self.place.along(axis, k)
-                for i in OTHERS:
-                    part = self.d.at[self.place.along(X, i)[0], self.place.core, rows, self.columns(u)]
-                    send(part, part, self.snd.at[Y, u], self.rcv.at[Y, u], to)
-
-    def start_d(self, u):
-        self.some(u, 2 * 3 * self.QUARTER, self.rcv, Y)
-        mine = self.d.at[self.place.at[X], self.place.core, :, self.columns(u)]
-        pairs = [(self.source.at[:, self.columns(u)], mine)]
-        for i in OTHERS:
-            pairs.append((self.d.at[self.place.along(X, i)[0], self.place.core, :, self.columns(u)],) * 2)
-        for src, dst in pairs:
-            send(src, dst, self.snd.at[Z, u], self.rcv.at[Z, u], self.place.partner())
-
-    def ready(self, u):
-        self.whole(u, self.rcv)
-
-    def finish(self):
-        self.load.wait()
-        self.store.start()
-        loop(self.UNITS, self.ready)
-
         def one(u):
-            self.some(u, self.ALONE + 2 * self.QUARTER, self.snd, X)
-            self.some(u, 2 * 3 * self.QUARTER, self.snd, Y)
-            self.whole(u, self.snd)
-
-        loop(self.UNITS, one)
-        self.store.wait()
+            for stage in self.STAGES:
+                self.came(stage, u, self.snd)
+
+        loop(self.units, one)
+
+
+class Gather(Fetch):
+    name, units, alone, quarter, all_rows = "g_", LAYERS * CHUNKS, 32, 16, ROWS
+
+    def block(self, u, chips, rows, half=ALL):
+        return self.w.at[u // CHUNKS, lax.rem(u, CHUNKS), half, chips, self.place.core, rows]
+
+    def mine(self, u, rows):
+        return self.source.at[u // CHUNKS, :, rows, at(lax.rem(u, CHUNKS), N)]
+
+
+class DownGather(Fetch):
+    parted = 5
+    name, units, alone, quarter, all_rows = "d_", LAYERS * parted, 64, 48, ROWS_DOWN
+
+    def columns(self, u, half=None):
+        u, n = lax.rem(u, self.parted), D // self.parted
+        return at(u, n) if half is None else at(2 * u + half, n // 2)
+
+    def block(self, u, chips, rows, half=None):
+        return self.w.at[u // self.parted, chips, self.place.core, rows, self.columns(u, half)]
+
+    def mine(self, u, rows):
+        return self.source.at[u // self.parted, rows, self.columns(u)]
+
+
+def chunk_of(place, w, j, into, semaphore):
+    return [pltpu.make_async_copy(w.at[j, :, k], into.at[:, place.along(X, k)[0]], semaphore) for k in range(RING)]
+
+
+def hidden_rows(place, d, j, into, semaphore):
+    for i in range(N // LANES):
+        n = j * (N // LANES) + i
+        k = lax.rem(n // CHUNKS + RING - place.at[X], RING)
+        yield pltpu.make_async_copy(d.at[k, at(lax.rem(n, CHUNKS), LANES)], into.at[at(i, LANES)], semaphore)
 
 
 class Sum:
@@ -294,9 +268,8 @@
                 q[u, 0, i] = t.astype(bf16)
             self.pass_on(2, u, k, ORDERS[k][2], lambda i, n, q=q, r=r: (q.at[u, 0, i], r.at[u, n]))
 
-    def lines(self, u, k):
-        _, y, z = self.place.at
-        return [self.ga.at[(u, y, to) + self.cuts[k]] for to in (z, ALL)]
+    def line(self, u, z):
+        return self.ga.at[u, self.place.at[Y], z]
 
     def add3(self, u):
         _, y, z = self.place.at
@@ -304,30 +277,25 @@
             arrive(r.at[u], self.sem("rcv", 2, u, k))
             t = two[self.place.at[ORDERS[k][2]]] + r[u, 0].astype(f32) + r[u, 1].astype(f32) + r[u, 2].astype(f32)
             self.ga[(u, y, z) + self.cuts[k]] = t.astype(bf16)
-            mine, _ = self.lines(u, k)
-            self.pass_on(3, u, k, Z, lambda q, n, mine=mine: (mine, mine))
-
-    def three(self, u, k, name, stage):
-        at = (u, pl.ds(0, 3), 0) if stage == 3 else (u, pl.ds(0, 3), ALL)
-        arrive(self.ga.at[at + self.cuts[k]], self.sem(name, stage, u, k))
+        self.pass_on(3, u, 0, Z, lambda q, n: [self.line(u, z)] * 2)
+
+    def three(self, u, name, stage):
+        arrive(self.ga.at[u, pl.ds(0, 3), 0 if stage == 3 else ALL], self.sem(name, stage, u, 0))
 
     def gather(self, u):
-        for k in AXES:
-            self.three(u, k, "rcv", 3)
-            _, line = self.lines(u, k)
-            self.pass_on(4, u, k, Y, lambda q, n, line=line: (line, line))
+        self.three(u, "rcv", 3)
+        self.pass_on(4, u, 0, Y, lambda q, n: [self.line(u, ALL)] * 2)
 
     def gathered(self, u):
-        for k in AXES:
-            self.three(u, k, "rcv", 4)
+        self.three(u, "rcv", 4)
 
     def finish(self):
         def one(u):
             for k, parts in self.refs("p", "q", "r"):
                 for stage, part in enumerate(parts):
                     arrive(part.at[u], self.sem("snd", stage, u, k))
-                for stage in (3, 4):
-                    self.three(u, k, "snd", stage)
+            for stage in (3, 4):
+                self.three(u, "snd", stage)
 
         loop(self.units, one)
 
@@ -524,259 +492,239 @@
 GATHERED = (CHUNKS, 2, RING, CORES, ROWS, N)
 
 
-def first_kernel(x, w_gate, w_up, w_down, a_out, hid_out, gu_out, d_out, *scratch, names):
+EARLY = gate_up_sum("e_", 3)
+LATE = gate_up_sum("l_", CHUNKS - EARLY.units, CHUNKS - EARLY.units)
+
+
+SHORT = 256
+SECOND, THIRD = 11, 19
+
+
+def forward_kernel(x, dy_in, w_gate, w_up, w_down, a_out, hid_out, gu_out, w_out, d_out, h_out, hid1_out, dg_out, du_out, ga_out, s_out, oh_out, *scratch, names):
     refs = named(names, scratch)
-    a, hs, gs, xsem, asem, hsem, gsem = (refs[n] for n in ("a", "hs", "gs", "xsem", "asem", "hsem", "gsem"))
-    load = pltpu.make_async_copy(x, a, xsem)
-    load.start()
+    blocks, low, a, lsem = (refs[n] for n in ("blocks", "low", "a", "lsem"))
+    pairs = [(w.at[n], blocks.at[n, m]) for n in range(LAYERS) for m, w in enumerate((w_gate, w_up))] + [(w_down, low), (x, a)]
+    loads = [pltpu.make_async_copy(*pair, lsem.at[n]) for n, pair in enumerate(pairs)]
+    start(loads)
     place = Place()
     place.meet()
-    gather = Gather(place, refs, refs["w"], (w_gate, w_up), 0)
-    down = DownGather(place, refs, d_out, w_down, 0)
-    for j in range(3):
-        gather.start_x(j)
-    down.load.start()
-    load.wait()
+    gather = Gather(place, refs, w_out, blocks)
+    down = DownGather(place, refs, d_out, low)
+    wait(loads[:4])
+    loop(2, gather.start_x)
+    wait(loads[4:])
 
     def norm(i):
         a[at(i, 64)] = normed(a[at(i, 64)])
 
     loop(T // 64, norm)
-    keep = pltpu.make_async_copy(a, a_out, asem)
-    keep.start()
-
-    def outs(j, i):
-        return (
-            pltpu.make_async_copy(hs.at[i], hid_out.at[at(i, TILE), at(j, N)], hsem.at[i]),
-            pltpu.make_async_copy(gs.at[i], gu_out.at[j, :, at(i, TILE)], gsem.at[i]),
-        )
-
-    def compute(j):
-        gather.ready(j)
-
-        def tile(i):
-            when(j > 0, lambda: wait(outs(j, i)))
-            g, u = (jnp.dot(a[at(i, TILE)], gather.w[j, m].reshape(D, N), preferred_element_type=f32) for m in range(2))
-            gs[i, 0], gs[i, 1] = g, u
-            hs[i] = (g * jax.nn.sigmoid(g) * u).astype(bf16)
-            start(outs(j, i))
-
-        loop(T // TILE, tile)
-
-    def step(t):
+    gather.pass_x(0)
+    gather.start_x(2)
+
+    def fetches(t):
+        within(t - 1, CHUNKS, gather.start_d)
         within(t, CHUNKS, gather.start_yz)
+        within(t + 1, CHUNKS, gather.pass_x)
+        for stage, first, second in ((down.start_d, 6, 9), (down.start_yz, 5, 7), (down.pass_x, 4, 5), (down.start_x, 3, 3)):
+            within(t - first, down.parted, stage)
+            within(t - second - down.parted, down.parted, lambda u, stage=stage: stage(u + down.parted))
+        within(t - THIRD + 1, CHUNKS, lambda u: gather.start_yz(u + CHUNKS))
+        within(t - THIRD + 3, CHUNKS, lambda u: gather.pass_x(u + CHUNKS))
+        within(t - SECOND - 1, CHUNKS, lambda u: gather.start_x(u + CHUNKS))
         within(t + 3, CHUNKS, gather.start_x)
-        within(t - 1, CHUNKS, gather.start_d)
-        for stage, lag in ((down.start_x, 4), (down.start_yz, 6), (down.start_d, 7)):
-            within(t - lag, down.UNITS, stage)
-        within(t - 2, CHUNKS, compute)
-
-    loop(CHUNKS + down.UNITS, step)
-    down.finish()
-    gather.finish()
-    keep.wait()
-    for i in range(T // TILE):
-        wait(outs(CHUNKS - 1, i))
-
-
-def first(x, w_gate, w_up, w_down, collective_id):
-    scratch = dict(
-        Gather.scratch(),
-        **DownGather.scratch(),
-        w=pltpu.VMEM(GATHERED, bf16),
-        a=pltpu.VMEM((T, D), bf16),
-        hs=pltpu.VMEM((T // TILE, TILE, N), bf16),
-        gs=pltpu.VMEM((T // TILE, 2, TILE, N), f32),
-        xsem=sem(),
-        asem=sem(),
-        hsem=sem(2),
-        gsem=sem(2),
+
+    def load_chunk(u, wv, vsem):
+        gather.ready(u)
+        slot = lax.rem(u, 2)
+        start(chunk_of(place, w_out.at[u // CHUNKS], lax.rem(u, CHUNKS), wv.at[slot], vsem.at[slot]))
+
+    def layer0(wv, hs, gs, asem, vsem, hsem, gsem):
+        keep = pltpu.make_async_copy(a, a_out, asem)
+        keep.start()
+
+        def outs(j, i):
+            return (
+                pltpu.make_async_copy(hs.at[i], hid_out.at[at(i, TILE), at(j, N)], hsem.at[i]),
+                pltpu.make_async_copy(gs.at[i], gu_out.at[j, :, at(i, TILE)], gsem.at[i]),
+            )
+
+        def compute(j):
+            slot = lax.rem(j, 2)
+            arrive(wv.at[slot], vsem.at[slot])
+
+            def tile(i):
+                when(j > 0, lambda: wait(outs(j, i)))
+                g, u = (jnp.dot(a[at(i, TILE)], wv[slot, m].reshape(D, N), preferred_element_type=f32) for m in range(2))
+                gs[i, 0], gs[i, 1] = g, u
+                hs[i] = (g * jax.nn.sigmoid(g) * u).astype(bf16)
+                start(outs(j, i))
+                when((i == 0) & (j + 1 < CHUNKS), load_chunk, j + 1, wv, vsem)
+
+            loop(T // TILE, tile)
+
+        def step(t):
+            fetches(t)
+            when(t == 1, load_chunk, 0, wv, vsem)
+            within(t - 2, CHUNKS, compute)
+
+        loop(SECOND, step)
+        keep.wait()
+        for i in range(T // TILE):
+            wait(outs(CHUNKS - 1, i))
+
+    pl.run_scoped(
+        layer0,
+        pltpu.VMEM((2,) + GATHERED[1:], bf16),
+        pltpu.VMEM((T // TILE, TILE, N), bf16),
+        pltpu.VMEM((T // TILE, 2, TILE, N), f32),
+        *[sem()] + [sem(2)] * 3,
     )
-    outs = (shape(T, D), shape(T, F), shape(CHUNKS, 2, T, N, dtype=f32), shape(RING, CORES, ROWS_DOWN, D))
-    return call(first_kernel, "first", outs, scratch, collective_id, x, w_gate, w_up, w_down)
-
-
-SHORT = 512
-
-
-def second_kernel(x, hid, d, w_down, h_out, a_out, d1_out, *scratch, names):
-    refs = named(names, scratch)
-    dv, hv, xv, ho, ao, dsem, hsem, xsem, osem = (refs[n] for n in ("dv", "hv", "xv", "ho", "ao", "dsem", "hsem", "xsem", "osem"))
-
-    def loads(i, slot):
-        return (
-            pltpu.make_async_copy(hid.at[at(i, SHORT)], hv.at[slot], hsem.at[slot]),
-            pltpu.make_async_copy(x.at[at(i, SHORT)], xv.at[slot], xsem.at[slot]),
-        )
-
-    def stores(i, slot):
-        pairs = ((ho, h_out), (ao, a_out))
-        return [pltpu.make_async_copy(v.at[slot], out.at[at(i, SHORT)], osem.at[n, slot]) for n, (v, out) in enumerate(pairs)]
-
-    load = pltpu.make_async_copy(d, dv, dsem)
-    load.start()
-    start(loads(0, 0))
-    place = Place()
-    place.meet()
-    down = DownGather(place, refs, d1_out, w_down, 1)
-    down.load.start()
-    loop(down.UNITS, down.start_x)
-    load.wait()
-
-    def compute(i):
-        slot = lax.rem(i, 2)
-        wait(loads(i, slot))
-        when(i + 1 < T // SHORT, lambda: start(loads(i + 1, 1 - slot)))
-        when(i > 1, lambda: wait(stores(i, slot)))
-        h = xv[slot] + jnp.dot(hv[slot], dv[...].reshape(F, D), preferred_element_type=f32).astype(bf16)
-        ho[slot] = h
-        ao[slot] = normed(h)
-        start(stores(i, slot))
-
-    def step(t):
-        within(t, T // SHORT, compute)
-        within(t, down.UNITS, down.start_yz)
-        within(t - 1, down.UNITS, down.start_d)
-
-    loop(down.UNITS + 1, step)
-    down.finish()
-    for slot in range(2):
-        wait(stores(0, slot))
-
-
-def second(x, hid, d, w_down, collective_id):
-    pair = pltpu.VMEM((2, SHORT, D), bf16)
-    scratch = dict(
-        DownGather.scratch(),
-        dv=pltpu.VMEM((RING, CORES, ROWS_DOWN, D), bf16),
-        hv=pltpu.VMEM((2, SHORT, F), bf16),
-        xv=pair,
-        ho=pair,
-        ao=pair,
-        dsem=sem(),
-        hsem=sem(2),
-        xsem=sem(2),
-        osem=sem(2, 2),
+    loop(down.parted, down.ready)
+
+    def between(dv, hv, xv, dsem, hsem, xsem, osem):
+        def loads(i, slot):
+            return (
+                pltpu.make_async_copy(hid_out.at[at(i, SHORT)], hv.at[slot], hsem.at[slot]),
+                pltpu.make_async_copy(x.at[at(i, SHORT)], xv.at[slot], xsem.at[slot]),
+            )
+
+        def store(i, slot):
+            return pltpu.make_async_copy(xv.at[slot], h_out.at[at(i, SHORT)], osem.at[slot])
+
+        for k in range(RING):
+            pltpu.make_async_copy(d_out.at[0, k], dv.at[place.along(X, k)[0]], dsem).start()
+        start(loads(0, 0))
+        arrive(dv, dsem)
+
+        def step(i):
+            fetches(i + SECOND)
+            slot = lax.rem(i, 2)
+            wait(loads(i, slot))
+            when(i > 0, lambda: store(i, 1 - slot).wait())
+            when(i + 1 < T // SHORT, lambda: start(loads(i + 1, 1 - slot)))
+            h = xv[slot] + jnp.dot(hv[slot], dv[...].reshape(F, D), preferred_element_type=f32).astype(bf16)
+            xv[slot] = h
+            a[at(i, SHORT)] = normed(h)
+            store(i, slot).start()
+
+        loop(T // SHORT, step)
+        store(0, 1).wait()
+
+    pl.run_scoped(
+        between,
+        pltpu.VMEM((RING, CORES, ROWS_DOWN, D), bf16),
+        pltpu.VMEM((2, SHORT, F), bf16),
+        pltpu.VMEM((2, SHORT, D), bf16),
+        sem(),
+        *[sem(2)] * 3,
     )
-    outs = (shape(T, D), shape(T, D), shape(RING, CORES, ROWS_DOWN, D))
-    return call(second_kernel, "second", outs, scratch, collective_id, x, hid, d, w_down)
-
-
-EARLY = gate_up_sum("e_", 3)
-LATE = gate_up_sum("l_", CHUNKS - EARLY.units, CHUNKS - EARLY.units)
-
-
-def third_kernel(a_in, dy_in, d, w_gate, w_up, hid_out, dg_out, du_out, w_out, ga_out, s_out, oh_out, *scratch, names):
-    refs = named(names, scratch)
-    a, dy, dv, wv, side, lsem, dsem, vsem, osem, ksem = (refs[n] for n in ("a", "dy", "dv", "wv", "side", "lsem", "dsem", "vsem", "osem", "ksem"))
-    blocks = refs["blocks"]
-    pairs = ((w_gate.at[1], blocks.at[0]), (w_up.at[1], blocks.at[1]), (a_in, a), (dy_in, dy))
-    loads = [pltpu.make_async_copy(*pair, lsem.at[n]) for n, pair in enumerate(pairs)]
-    start(loads)
-
-    def operands(j):
-        slot = lax.rem(j, 2)
-        return (
-            pltpu.make_async_copy(d.at[at(j, N)], dv.at[slot], dsem.at[slot]),
-            pltpu.make_async_copy(w_out.at[j], wv.at[slot], vsem.at[slot]),
-        )
-
-    place = Place()
-    place.meet()
-    gather = Gather(place, refs, w_out, (w_gate, w_up), 1, blocks)
-    wait(loads[:2])
+    loop(down.parted, lambda u: down.ready(u + down.parted))
     s = refs["s"]
     total = EARLY.bind(place, refs, s)
-    grads = GateUp(place, refs, s, refs["come"])
-    for j in range(3):
-        gather.start_x(j)
-    wait(loads[2:])
-
-    def fetch(j):
-        gather.ready(j)
-        start(operands(j))
-
-    def outs(j):
-        return [pltpu.make_async_copy(side.at[n], out.at[:, at(j, N)], osem.at[n]) for n, out in enumerate((dg_out, du_out, hid_out))]
-
-    def leave(u):
-        late = u - EARLY.units
-        return (pltpu.make_async_copy(s.at[u], s_out.at[late], ksem.at[0]), pltpu.make_async_copy(grads.oh, oh_out.at[late], ksem.at[1]))
-
-    def join(u):
-        grads.join(u)
-
-        def go_on():
-            grads.keep(total, u)
-            total.start1(u)
-
-        when(u < EARLY.units, go_on)
-        when(u >= EARLY.units, lambda: start(leave(u)))
-
-    def compute(j):
-        slot = lax.rem(j, 2)
-        wait(operands(j))
-        when(j > 0, lambda: wait(outs(j)))
-
-        def tile(i):
-            rows = at(i, TILE)
-            g, u = (jnp.dot(a[rows], wv[slot, m].reshape(D, N), preferred_element_type=f32) for m in range(2))
-            by = lax.dot_general(dy[rows], dv[slot], BY_LAST, preferred_element_type=f32)
-            side[0, rows], side[1, rows], side[2, rows] = backward(by, g, u)
-
-        loop(T // TILE, tile)
-        start(outs(j))
-        within(j + 1, CHUNKS, fetch)
-        total.stages(j - 1)
-        within(j - 1, CHUNKS, join)
-        grads.multiply(j, a, (side.at[0], side.at[1]), lambda: when(j > EARLY.units, lambda: wait(leave(j - 1))))
-
-    def step(t):
-        within(t, CHUNKS, gather.start_yz)
-        within(t + 3, CHUNKS, gather.start_x)
-        within(t - 1, CHUNKS, gather.start_d)
-        when(t == 1, fetch, 0)
-        within(t - 2, CHUNKS, compute)
-
-    loop(CHUNKS + 2, step)
-    total.stages(CHUNKS - 1)
-    join(CHUNKS - 1)
-    total.stages(CHUNKS)
-    wait(leave(CHUNKS - 1))
-    grads.finish()
+
+    def layer1(dy, dv, wv, side, ysem, dsem, vsem, osem, ksem, **refs_grads):
+        grads = GateUp(place, refs_grads, s, refs["come"])
+        load = pltpu.make_async_copy(dy_in, dy, ysem)
+        load.start()
+
+        def fetch(j):
+            slot = lax.rem(j, 2)
+            start(hidden_rows(place, d_out.at[1].reshape(RING, WIDE, D), j, dv.at[slot], dsem.at[slot]))
+            load_chunk(j + CHUNKS, wv, vsem)
+
+        def outs(j):
+            return [pltpu.make_async_copy(side.at[n], out.at[:, at(j, N)], osem.at[n]) for n, out in enumerate((dg_out, du_out, hid1_out))]
+
+        def leave(u):
+            late = u - EARLY.units
+            return (pltpu.make_async_copy(s.at[u], s_out.at[late], ksem.at[0]), pltpu.make_async_copy(grads.oh, oh_out.at[late], ksem.at[1]))
+
+        def join(u):
+            grads.join(u)
+
+            def go_on():
+                grads.keep(total, u)
+                total.start1(u)
+
+            when(u < EARLY.units, go_on)
+            when(u >= EARLY.units, lambda: start(leave(u)))
+
+        gather.start_d(CHUNKS)
+        fetch(0)
+        load.wait()
+
+        def step(j):
+            fetches(j + THIRD)
+            slot = lax.rem(j, 2)
+            arrive(dv.at[slot], dsem.at[slot])
+            arrive(wv.at[lax.rem(j + CHUNKS, 2)], vsem.at[lax.rem(j + CHUNKS, 2)])
+            when(j > 0, lambda: wait(outs(j)))
+
+            def tile(i):
+                rows = at(i, TILE)
+                g, u = (jnp.dot(a[rows], wv[lax.rem(j + CHUNKS, 2), m].reshape(D, N), preferred_element_type=f32) for m in range(2))
+                by = lax.dot_general(dy[rows], dv[slot], BY_LAST, preferred_element_type=f32)
+                side[0, rows], side[1, rows], side[2, rows] = backward(by, g, u)
+
+            loop(T // TILE, tile)
+            start(outs(j))
+            within(j + 1, CHUNKS, lambda j: gather.start_d(j + CHUNKS))
+            total.stages(j - 1)
+            within(j - 1, CHUNKS, join)
+
+            def halfway():
+                when(j > EARLY.units, lambda: wait(leave(j - 1)))
+                within(j + 1, CHUNKS, fetch)
+
+            grads.multiply(j, a, (side.at[0], side.at[1]), halfway)
+
+        loop(CHUNKS, step)
+        total.stages(CHUNKS - 1)
+        join(CHUNKS - 1)
+        total.stages(CHUNKS)
+        wait(leave(CHUNKS - 1))
+        grads.finish()
+        wait(outs(CHUNKS - 1))
+
+    pl.run_scoped(
+        layer1,
+        pltpu.VMEM((T, D), bf16),
+        pltpu.VMEM((2, N, D), bf16),
+        pltpu.VMEM((2,) + GATHERED[1:], bf16),
+        pltpu.VMEM((3, T, N), bf16),
+        *[sem()] + [sem(2)] * 2 + [sem(3), sem(2)],
+        **GateUp.scratch(),
+    )
+    keep = pltpu.make_async_copy(total.ga, ga_out, lsem.at[0])
+    keep.start()
     gather.finish()
+    down.finish()
     total.finish()
-    wait(outs(CHUNKS - 1))
-    keep = pltpu.make_async_copy(total.ga, ga_out, ksem.at[0])
-    keep.start()
     keep.wait()
 
 
-def third(a, dy, d, w_gate, w_up, collective_id):
+def forward(x, dy, w_gate, w_up, w_down, collective_id):
     pieces = (RING, RING, RING, ROWS // 2, LANES)
     early = EARLY.scratch()
     del early["e_s"]
     scratch = dict(
         Gather.scratch(),
-        **GateUp.scratch(),
+        **DownGather.scratch(),
         **early,
         s=pltpu.VMEM((CHUNKS,) + pieces, bf16),
         come=sem(CHUNKS),
         a=pltpu.VMEM((T, D), bf16),
-        dy=pltpu.VMEM((T, D), bf16),
-        dv=pltpu.VMEM((2, N, D), bf16),
-        wv=pltpu.VMEM((2,) + GATHERED[1:], bf16),
-        side=pltpu.VMEM((3, T, N), bf16),
-        blocks=pltpu.VMEM((2, ROWS, F), bf16),
-        lsem=sem(4),
-        dsem=sem(2),
-        vsem=sem(2),
-        osem=sem(3),
-        ksem=sem(2),
+        blocks=pltpu.VMEM((LAYERS, 2, ROWS, F), bf16),
+        low=pltpu.VMEM((LAYERS, ROWS_DOWN, D), bf16),
+        lsem=sem(6),
     )
-    outs = [shape(T, F)] * 3 + [shape(*GATHERED), shape(EARLY.units, RING, RING, ROWS // 2, LANES)]
+    outs = [shape(T, D), shape(T, F), shape(CHUNKS, 2, T, N, dtype=f32), shape(LAYERS, *GATHERED), shape(LAYERS, RING, CORES, ROWS_DOWN, D)]
+    outs += [shape(T, D)] + [shape(T, F)] * 3 + [shape(EARLY.units, RING, RING, ROWS // 2, LANES)]
     outs += [shape(LATE.units, *pieces), shape(LATE.units, *pieces, dtype=f32)]
-    return call(third_kernel, "third", outs, scratch, collective_id, a, dy, d.reshape(F, D), w_gate, w_up)
+    return call(forward_kernel, "forward", outs, scratch, collective_id, x, dy, w_gate, w_up, w_down)
+
+
+TALL_TILE = 512
 
 
 def fourth_kernel(hid, dy_in, dg, du, w, h, s_in, oh_in, dh_out, ga_out, gd_out, *scratch, names):
@@ -796,9 +744,9 @@
 
     def late_stages(t):
         late.stages(t)
-        within(t, late.units, late.start1)
-
-    late_stages(0)
+        within(t + 1, late.units, late.start1)
+
+    loop(2, late.start1)
 
     def multiply_down(**refs_down):
         down = Down(place, low, refs_down, hid, refs["come"])
@@ -810,21 +758,26 @@
 
     def multiply_back(gv, wv, acc, hv, gsem, hsem):
         def loads(j, slot):
-            yield pltpu.make_async_copy(w.at[j], wv.at[slot], gsem.at[slot, 2])
             for n, side in enumerate((dg, du)):
                 yield pltpu.make_async_copy(side.at[:, at(j, N)], gv.at[slot, n], gsem.at[slot, n])
 
-        start(loads(0, 0))
+        def fetch(j):
+            slot = lax.rem(j, 2)
+            start(loads(j, slot))
+            start(chunk_of(place, w.at[1], j, wv.at[slot], gsem.at[slot, 2]))
+
+        fetch(0)
 
         def step(j):
             slot = lax.rem(j, 2)
             wait(loads(j, slot))
-            when(j + 1 < CHUNKS, lambda: start(loads(j + 1, 1 - slot)))
+            arrive(wv.at[slot], gsem.at[slot, 2])
+            within(j + 1, CHUNKS, fetch)
             late_stages(j + 1)
             low.stages(j)
 
             def tile(i):
-                rows = at(i, SHORT)
+                rows = at(i, TALL_TILE)
                 by, more = (lax.dot_general(gv[slot, m, rows], wv[slot, m].reshape(D, N), BY_LAST, preferred_element_type=f32) for m in range(2))
                 by += more
 
@@ -837,7 +790,7 @@
                 when(j == 0, first_time)
                 when(j > 0, again)
 
-            loop(T // SHORT, tile)
+            loop(T // TALL_TILE, tile)
 
         loop(CHUNKS, step)
 
@@ -846,7 +799,7 @@
             return pltpu.make_async_copy(h.at[at(i, 256)], hv.at[slot], hsem.at[slot])
 
         tile_of_h(0).start()
-        late_stages(CHUNKS + 1)
+        late.stages(CHUNKS + 1)
 
         def norm(i):
             tile_of_h(i).wait()
@@ -914,20 +867,21 @@
         down.run(dy)
 
     pl.run_scoped(multiply_down, **Down.scratch())
-    tiles, ahead = T // SHORT, 3
+    tiles, ahead = T // TALL_TILE, 3
 
     def multiply_gates(a, dv, gv, side, asem, dsem, gsem, **refs_grads):
         grads = GateUp(place, refs_grads, total.s, refs["arrived"])
         load_a = pltpu.make_async_copy(a_in, a, asem)
 
         def rows_of_d(j):
-            return pltpu.make_async_copy(d.at[at(j, N)], dv, dsem)
+            start(hidden_rows(place, d.at[0], j, dv, dsem))
 
         def tile_of_gu(n):
             slot = lax.rem(n, ahead)
-            return pltpu.make_async_copy(gu.at[n // tiles, :, at(lax.rem(n, tiles), SHORT)], gv.at[slot], gsem.at[slot])
-
-        start([rows_of_d(0), load_a] + [tile_of_gu(n) for n in range(ahead)])
+            return pltpu.make_async_copy(gu.at[n // tiles, :, at(lax.rem(n, tiles), TALL_TILE)], gv.at[slot], gsem.at[slot])
+
+        rows_of_d(0)
+        start([load_a] + [tile_of_gu(n) for n in range(ahead)])
 
         def join(u):
             grads.join(u)
@@ -935,17 +889,17 @@
             total.start1(u)
 
         def back(j):
-            rows_of_d(j).wait()
+            arrive(dv, dsem)
 
             def tile(i):
                 n = j * tiles + i
                 tile_of_gu(n).wait()
-                by = lax.dot_general(dy[at(i, SHORT)], dv[...], BY_LAST, preferred_element_type=f32)
-                side[0, at(i, SHORT)], side[1, at(i, SHORT)], _ = backward(by, gv[lax.rem(n, ahead), 0], gv[lax.rem(n, ahead), 1])
+                by = lax.dot_general(dy[at(i, TALL_TILE)], dv[...], BY_LAST, preferred_element_type=f32)
+                side[0, at(i, TALL_TILE)], side[1, at(i, TALL_TILE)], _ = backward(by, gv[lax.rem(n, ahead), 0], gv[lax.rem(n, ahead), 1])
                 when(n + ahead < CHUNKS * tiles, lambda: tile_of_gu(n + ahead).start())
 
             loop(tiles, tile)
-            when(j + 1 < CHUNKS, lambda: rows_of_d(j + 1).start())
+            within(j + 1, CHUNKS, rows_of_d)
 
         def step(t):
             within(t, CHUNKS, back)
@@ -962,7 +916,7 @@
         multiply_gates,
         pltpu.VMEM((T, D), bf16),
         pltpu.VMEM((N, D), bf16),
-        pltpu.VMEM((ahead, 2, SHORT, N), f32),
+        pltpu.VMEM((ahead, 2, TALL_TILE, N), f32),
         pltpu.VMEM((2, T, N), bf16),
         sem(),
         sem(),
@@ -1024,7 +978,7 @@
         q_rcv=sem(),
     )
     outs = [shape(CHUNKS, RING, RING, ROWS // 2, LANES), shape(*Down.PIECE), shape(8, LANES, dtype=f32)]
-    return call(fifth_kernel, "fifth", outs, scratch, collective_id, hid, dy, a, d.reshape(F, D), gu, *layer1)
+    return call(fifth_kernel, "fifth", outs, scratch, collective_id, hid, dy, a, d.reshape(LAYERS, RING, WIDE, D), gu, *layer1)
 
 
 SLOTS = 4
@@ -1067,10 +1021,10 @@
         w[part] = (old - 0.02 * (new_m * lax.rsqrt(new_v + 1e-8) + 0.1 * old)).astype(bf16)
         m[part], v[part] = new_m, new_v
 
+    def begin(transfer):
+        loop(SLOTS - 1, lambda n: transfer(n, start, weights, True, 0))
+
     def run(steps, transfer, body):
-        for n in range(SLOTS - 1):
-            transfer(jnp.int32(n), start, weights, True, 0)
-
         def step(n):
             transfer(n, wait, weights, True, 0)
             body(n, lax.rem(n, SLOTS))
@@ -1083,10 +1037,11 @@
 
     def gate_step(n, slot):
         def of(g):
-            for j in range(CHUNKS):
+            def chunk(j):
                 for y in range(RING):
-                    columns = slice(j * N + y * LANES, j * N + (y + 1) * LANES)
-                    adamw(slot, ("gw", "gm", "gv"), (ALL, columns), g[j, y, lax.rem(n, RING)])
+                    adamw(slot, ("gw", "gm", "gv"), (ALL, at(j * RING + y, LANES)), g[j, y, lax.rem(n, RING)])
+
+            loop(CHUNKS, chunk)
 
         when(n < RING, of, g0)
         when(n >= RING, of, g1)
@@ -1102,6 +1057,8 @@
         when(n < 2, of, d0)
         when(n >= 2, of, d1)
 
+    begin(gates)
+    begin(downs)
     wait(loads[1:])
     run(LAYERS * RING, gates, gate_step)
     run(LAYERS * 2, downs, down_step)
@@ -1122,11 +1079,9 @@
     def step(x, dy, *arrays):
         w_gate, w_up, w_down = arrays[:3]
         x, dy = x[0], dy[0]
-        a0, hid0, gu0, d0 = first(x, w_gate, w_up, w_down, 0)
-        h1, a1, d1 = second(x, hid0, d0, w_down, 1)
-        hid1, dg1, du1, w1, early, s, oh = third(a1, dy, d1, w_gate, w_up, 2)
-        dh1, late, down1 = fourth(hid1, dy, dg1, du1, w1, h1, s, oh, 3)
-        both0, down0, total = fifth(hid0, dh1, a0, d0, gu0, early, late, down1, collective_id=4)
+        a0, hid0, gu0, w, d, h1, hid1, dg1, du1, early, s, oh = forward(x, dy, w_gate, w_up, w_down, 0)
+        dh1, late, down1 = fourth(hid1, dy, dg1, du1, w, h1, s, oh, 1)
+        both0, down0, total = fifth(hid0, dh1, a0, d, gu0, early, late, down1, collective_id=2)
         return tuple(sixth(total, (early, late, down1, both0, down0), arrays))
 
     states, cut = P(("rep", "r", "s"), None, None), P(None, "s", None)

time: 596 us -> 576 us (0.966)
  Pallas kernels: 589 us -> 569 us
    pallas_call x6 -> x4, Pallas kernels: 589 us -> 569 us  [call(): pl.pallas_call(functools.partial(kernel, names=tuple(scratch)), out_shape...]
where the time goes in v3:
time: 576 us; the launch traced here: 570 us
  Pallas kernels  569 us (99%)
    pallas_call x4, Pallas kernels, call(): pl.pallas_call(functools.partial(kernel, names=tuple(scratch)), out_shape...  569 us

profile of v3, /device:TPU:1, one launch (start us, length us, event | category | flops | bytes accessed | tf_op | source)
XLA Modules:
  0.0 570.4 jit_solution(13207876857928013569)
XLA Ops:
  0.6 248.1 %forward.1 = (bf16[2048,1280]{1,0:T(8,128)(2,1)}, bf16[2048,3584]{1,0:T(8,128)(2,1)}, f32[7,2,2048,512]{3,2,1,0:T(8,128)}, bf16[2,7,2,4,2,160,512]{6,5,4,3,2,1,0...) custom-call(bf16[2048,1280]{1,0:T(8,128)(2,1)} %bitcast.6, ...), custom_call_target="tpu_custom_call" | custom-call | tf_op jit(solution)/shard_map/forward/pallas_call | solution.py:473
  248.7 120.1 %fourth.1 = (bf16[2048,1280]{1,0:T(8,128)(2,1)}, bf16[4,4,4,80,128]{4,3,2,1,0:T(8,128)(2,1)}, bf16[4,4,56,640]{3,2,1,0:T(8,128)(2,1)}) custom-call(bf16[2048,3584]{1,0:T(8,128)(2,1)} %get-tuple-element.28.hid, bf16[2048,1280]{1,0:T(8,128)(2,1)} %bitcast.4, bf16[2048,3584]{1,0:T(8,128)(2,1)} %get-tuple-element.29.dg, ...), custom_call_target="tpu_custom_call" | custom-call | tf_op jit(solution)/shard_map/fourth/pallas_call | solution.py:473
  368.8 172.9 %fifth.1 = (bf16[7,4,4,80,128]{4,3,2,1,0:T(8,128)(2,1)}, bf16[4,4,56,640]{3,2,1,0:T(8,128)(2,1)}, f32[8,128]{1,0:T(8,128)}) custom-call(bf16[2048,3584]{1,0:T(8,128)(2,1)} %get-tuple-element.27.hid, bf16[2048,1280]{1,0:T(8,128)(2,1)} %get-tuple-element.35.dy_in, bf16[2048,1280]{1,0:T(8,128)(2,1)} %get-tuple-element.36.a_in, ...), custom_call_target="tpu_custom_call" | custom-call | tf_op jit(solution)/shard_map/fifth/pallas_call | solution.py:473
  541.7 28.2 %sixth.1 = (bf16[2,160,3584]{2,1,0:T(8,128)(2,1)}, bf16[2,160,3584]{2,1,0:T(8,128)(2,1)}, bf16[2,448,1280]{2,1,0:T(8,128)(2,1)}, f32[2,160,3584]{2,1,0:T(8,128)}...) custom-call(f32[8,128]{1,0:T(8,128)} %get-tuple-element.42.args_0_, ...), custom_call_target="tpu_custom_call" | custom-call | tf_op jit(solution)/shard_map/sixth/pallas_call | solution.py:473
